TPU v7x, 32 devices: a whole 2x2x4 slice. The times are simulated.
32 devices in a mesh: slab: 8 (over y, x, core), atom: 4 (over z).
Axes of the slice: x: 2, y: 2, z: 4, core: 2. Of those that a mesh axis runs over, the one named last changes fastest.
Arguments:
- cells: int32 [3, 512, 512], P(None, 'slab', 'atom'), may hold values from 0 to 255, as said below
- fractions: float32 [3, 512, 512], P(None, 'slab', 'atom'), may hold values from 0 to 1
- charges: float32 [512, 512], P('slab', 'atom'), may hold values from -3 to 3
- counts: int32 [512, 4], P('slab', 'atom'), may hold values from 1 to 128, as said below
- box: float32 [3], replicated, may hold values from 192 to 243.2
Outputs:
- kfield: float32 [2, 256, 256, 256], P(None, 'slab', 'atom')
- totals: float32 [7], replicated
Inputs may be any that keep to these rules, and one draw needn't show every extreme that they name: `cells`: for row r (tile r mod 64 of slab r div 64) every slot's z cell lies in the 32 planes from (r div 64) * 32 and its y cell in the 4 rows from (r mod 64) * 4; x anywhere. `counts`: live slots are the first ones of a tile's 128; some tile is full in every draw.
All inputs are finite; a program needn't handle non-finite values.
Results may differ from a plain program's by a relative error of at most 0.000078.
Values sent between devices are 32-bit elements; how exact they have to be, the bound alone decides.
No kernel may reach another device: no remote copies, remote signals or barrier semaphores. Data moves between devices by JAX's collectives and lax.ppermute only.
A program may use at most 192 MiB of HBM per device.

v0:
```python
import math

import jax
import jax.numpy as jnp
from jax import lax
from jax.sharding import PartitionSpec as P

K = 256
TILES = 64
SLOTS = 128


ewald_beta = 1.25
highest = lax.Precision.HIGHEST


def from_behind(x, axis, by):
    count = lax.axis_size(axis)
    return lax.ppermute(x, axis, [(i, (i + by) % count) for i in range(count)])


def spline_weights(frac):
    prior = [jnp.ones_like(frac)]
    for order in range(2, 7):
        nxt = []
        for i in range(order):
            point = frac + i
            here = prior[i] if i < order - 1 else jnp.zeros_like(frac)
            lower = prior[i - 1] if i > 0 else jnp.zeros_like(frac)
            nxt.append((point * here + (order - point) * lower) / (order - 1))
        prior = nxt
    return prior


def dft_tables(length):
    index = jnp.arange(length, dtype=jnp.int32)
    phase = index[:, None] * index[None, :] % length
    angle = phase.astype(jnp.float32) * (2.0 * math.pi / length)
    return (jnp.cos(angle), jnp.sin(angle))


def moduli(index):
    angle = (index % K).astype(jnp.float32) * (2.0 * math.pi / K)
    denom = 66.0 + 52.0 * jnp.cos(angle) + 2.0 * jnp.cos(2.0 * angle)
    return (120.0 / denom) ** 2


def spread(cells, fractions, charges, counts, depth, rows_tile):
    tiles, slots = charges.shape
    lead = (depth + 1) // depth
    above = (depth + 2) // depth
    planes = (lead + 1 + above) * depth
    blocks = 1 + (rows_tile + 4) // rows_tile
    span = blocks * rows_tile
    live = (jnp.arange(slots, dtype=jnp.int32)[None, :] < counts).astype(jnp.float32)
    weight = charges * live
    along_z = spline_weights(fractions[0])
    along_y = spline_weights(fractions[1])
    along_x = spline_weights(fractions[2])
    start_z = cells[0] % depth + lead * depth + 3
    start_y = cells[1] % rows_tile + 5
    plane_ids = jnp.arange(planes, dtype=jnp.int32)
    row_ids = jnp.arange(span, dtype=jnp.int32)
    col_ids = jnp.arange(K, dtype=jnp.int32)
    table_z = jnp.zeros((tiles, slots, planes), jnp.float32)
    table_y = jnp.zeros((tiles, slots, span), jnp.float32)
    table_x = jnp.zeros((tiles, slots, K), jnp.float32)
    for i in range(6):
        table_z = table_z + jnp.where(
            plane_ids == (start_z - i)[..., None], along_z[i][..., None], 0.0
        )
        table_y = table_y + jnp.where(
            row_ids == (start_y - i)[..., None], along_y[i][..., None], 0.0
        )
        table_x = table_x + jnp.where(
            col_ids == ((cells[2] + 3 - i) % K)[..., None], along_x[i][..., None], 0.0
        )
    weighted_z = weight[..., None] * table_z
    summed = jnp.zeros((tiles, planes, rows_tile, K), jnp.float32)
    for shift_by in range(blocks):
        rows_part = table_y[..., shift_by * rows_tile : (shift_by + 1) * rows_tile]
        left = (weighted_z[..., :, None] * rows_part[..., None, :]).reshape(
            tiles, slots, planes * rows_tile
        )
        product = jnp.einsum("tsa,tsx->tax", left, table_x, precision=highest)
        product = product.reshape(tiles, planes, rows_tile, K)
        summed = summed + jnp.roll(product, shift_by, axis=0)
    grid = jnp.transpose(summed, (1, 0, 2, 3)).reshape(planes, tiles * rows_tile, K)
    return jnp.roll(grid, -2, axis=1)[None]


def fold_planes(data, depth):
    lead = (depth + 1) // depth
    above = (depth + 2) // depth
    own = data[:, lead * depth : (lead + 1) * depth]
    step = 1
    piece = data[:, (lead - step) * depth : (lead - step + 1) * depth]
    own = own + from_behind(piece, "slab", -step)
    step = 1
    piece = data[:, (lead + step) * depth : (lead + step + 1) * depth]
    own = own + from_behind(piece, "slab", step)
    return own


def transform_x(data, cosine, sine):
    real_in = data[0]
    real_part = jnp.dot(real_in, cosine, precision=highest)
    imag_part = -jnp.dot(real_in, sine, precision=highest)
    return jnp.stack([real_part, imag_part])


def transform(data, cosine, sine, form):
    real_in, imag_in = (data[0], data[1])
    real_part = jnp.einsum(form, real_in, cosine, precision=highest) + jnp.einsum(
        form, imag_in, sine, precision=highest
    )
    imag_part = jnp.einsum(form, imag_in, cosine, precision=highest) - jnp.einsum(
        form, real_in, sine, precision=highest
    )
    return jnp.stack([real_part, imag_part])


def reduce_shards(data):
    return lax.psum_scatter(data, "atom", scatter_dimension=2, tiled=True)


def body(cells, fractions, charges, counts, box):
    slabs = lax.axis_size("slab")
    shards = lax.axis_size("atom")
    depth = K // slabs
    quarter = K // shards
    rows_tile = K // TILES
    cosine, sine = dft_tables(K)
    data = spread(cells, fractions, charges, counts, depth, rows_tile)
    data = reduce_shards(fold_planes(data, depth))
    data = transform_x(data, cosine, sine)
    data = lax.all_to_all(data, "atom", split_axis=3, concat_axis=2, tiled=True)
    data = transform(data, cosine, sine, "zyx,yk->zkx")
    data = lax.all_to_all(data, "slab", split_axis=2, concat_axis=1, tiled=True)
    data = transform(data, cosine, sine, "zyx,zk->yxk")
    real_part, imag_part = (data[0], data[1])
    index_z = jnp.arange(K, dtype=jnp.int32)
    index_y = lax.axis_index("slab") * depth + jnp.arange(depth, dtype=jnp.int32)
    index_x = lax.axis_index("atom") * quarter + jnp.arange(quarter, dtype=jnp.int32)

    def folded(index):
        return jnp.where(index < K // 2, index, index - K).astype(jnp.float32)

    m_z = (folded(index_z) / box[0])[None, None, :]
    m_y = (folded(index_y) / box[1])[:, None, None]
    m_x = (folded(index_x) / box[2])[None, :, None]
    msq = m_z * m_z + m_y * m_y + m_x * m_x
    anchor = (
        (index_y[:, None, None] == 0)
        & (index_x[None, :, None] == 0)
        & (index_z[None, None, :] == 0)
    )
    safe = jnp.where(anchor, 1.0, msq)
    volume = box[0] * box[1] * box[2]
    spline_part = (
        moduli(index_z)[None, None, :]
        * moduli(index_y)[:, None, None]
        * moduli(index_x)[None, :, None]
    )
    theta = jnp.exp(-math.pi**2 * safe / ewald_beta**2) * spline_part / (math.pi * volume * safe)
    theta = jnp.where(anchor, 0.0, theta)
    kfield = jnp.stack([theta * real_part, theta * imag_part])
    half = 0.5 * theta * (real_part * real_part + imag_part * imag_part)
    factor = 2.0 * (1.0 + math.pi**2 * safe / ewald_beta**2) / safe
    local_terms = jnp.stack(
        [
            jnp.sum(half),
            jnp.sum(half * (1.0 - factor * m_z * m_z)),
            jnp.sum(half * (1.0 - factor * m_y * m_y)),
            jnp.sum(half * (1.0 - factor * m_x * m_x)),
            jnp.sum(half * (-factor * m_z * m_y)),
            jnp.sum(half * (-factor * m_z * m_x)),
            jnp.sum(half * (-factor * m_y * m_x)),
        ]
    )
    count = TILES * slabs * SLOTS * shards
    totals = lax.psum(local_terms, ("slab", "atom")) / count
    return (kfield, totals)


def solution(mesh):
    in_specs = (
        P(None, "slab", "atom"),
        P(None, "slab", "atom"),
        P("slab", "atom"),
        P("slab", "atom"),
        P(),
    )
    out_specs = (P(None, "slab", "atom", None), P())
    return jax.shard_map(body, mesh=mesh, in_specs=in_specs, out_specs=out_specs, check_vma=False)
```

profile of v0, /device:TPU:0, one launch (start us, length us, event | category | flops | bytes accessed | tf_op | source)
XLA Modules:
  0.0 1118.0 jit_solution(1102384864975360654)
XLA Ops:
  13.0 14.0 %broadcast_multiply_fusion = (f32[64,128,96,4]{1,3,2,0:T(4,128)S(1)}, f32[64,128,96,4]{1,3,2,0:T(4,128)}, f32[64,128,96,4]{1,3,2,0:T(4,128)}) fusion(f32[64,128,4]{1,2,0:T(4,128)S(1)} %get-tuple-element.25, f32[64,128,96]{1,2,0:T(8,128)S(1)} %add_multiply_fusion, f32[64,128,4]{1,2,0:T(4,128)S(1)} %get-tuple-element.26, f32[64,128,4]{1,2,0:T(4,128)S(1)} %get-tuple-element.27), kind=kLoop, calls=%fused_computation.14 | loop fusion | flops 9437184 | bytes 41287680 | tf_op jit(solution)/shard_map/mul | solution.py:82
  26.9 49.0 %fusion.4 = f32[64,384,256]{2,1,0:T(8,128)S(1)} fusion(f32[64,128,384]{1,2,0:T(8,128)} %bitcast.667, f32[64,128]{1,0:T(8,128)S(1)} %get-tuple-element.54, s32[64,128]{1,0:T(8,128)S(1)} %get-tuple-element.40, f32[64,128]{1,0:T(8,128)S(1)} %get-tuple-element.55, s32[64,128]{1,0:T(8,128)S(1)} %get-tuple-element.39, f32[64,128]{1,0:T(8,128)S(1)} %get-tuple-element.60, ...), kind=kOutput, calls=%fused_computation.21 | convolution fusion | flops 9699328000 | bytes 38141952 | tf_op jit(solution)/shard_map/tsa,tsx->tax/dot_general | solution.py:85
  76.0 10.3 slice.137
  91.7 46.8 %fusion.3 = f32[64,384,256]{2,1,0:T(8,128)S(1)} fusion(f32[64,128,384]{1,2,0:T(8,128)S(1)} %bitcast.666, f32[64,128]{1,0:T(8,128)S(1)} %get-tuple-element.54, s32[64,128]{1,0:T(8,128)S(1)} %get-tuple-element.40, f32[64,128]{1,0:T(8,128)S(1)} %get-tuple-element.55, s32[64,128]{1,0:T(8,128)S(1)} %get-tuple-element.39, f32[64,128]{1,0:T(8,128)S(1)} %get-tuple-element.60, ...), kind=kOutput, calls=%fused_computation.20 | convolution fusion | flops 9699328000 | bytes 38141952 | tf_op jit(solution)/shard_map/tsa,tsx->tax/dot_general | solution.py:85
  138.6 8.6 slice.140
  147.1 28.3 %slice.119 = f32[63,96,4,256]{3,2,1,0:T(4,128)} reshape(f32[63,384,256]{2,1,0:T(8,128)} %slice.137) | data formatting | bytes 49545216 | tf_op jit(solution)/shard_map/jit(_roll_static)/slice | solution.py:87
  175.6 28.2 %slice.124 = f32[62,96,4,256]{3,2,1,0:T(4,128)} reshape(f32[62,384,256]{2,1,0:T(8,128)} %slice.140) | data formatting | bytes 48758784 | tf_op jit(solution)/shard_map/jit(_roll_static)/slice | solution.py:87
  204.0 37.6 %fusion.5 = f32[64,384,256]{2,1,0:T(8,128)} fusion(f32[64,128,384]{1,2,0:T(8,128)} %bitcast.665, f32[64,128]{1,0:T(8,128)S(1)} %get-tuple-element.54, s32[64,128]{1,0:T(8,128)S(1)} %get-tuple-element.40, f32[64,128]{1,0:T(8,128)S(1)} %get-tuple-element.55, s32[64,128]{1,0:T(8,128)S(1)} %get-tuple-element.39, f32[64,128]{1,0:T(8,128)S(1)} %get-tuple-element.60, ...), kind=kOutput, calls=%fused_computation.22 | convolution fusion | flops 9699328000 | bytes 38141952 | tf_op jit(solution)/shard_map/tsa,tsx->tax/dot_general | solution.py:85
  241.6 28.2 %reshape.1139 = f32[64,96,4,256]{3,2,1,0:T(4,128)} reshape(f32[64,384,256]{2,1,0:T(8,128)} %fusion.5) | data formatting | bytes 50331648 | tf_op jit(solution)/shard_map/reshape | solution.py:86
  269.8 33.5 %fusion.1 = f32[96,64,4,256]{3,2,0,1:T(4,128)} fusion(f32[64,96,4,256]{3,2,1,0:T(4,128)} %reshape.1139, f32[63,96,4,256]{3,2,1,0:T(4,128)} %slice.119, f32[1,96,4,256]{3,2,1,0:T(4,128)S(1)} %slice.117, f32[62,96,4,256]{3,2,1,0:T(4,128)} %slice.124, f32[2,96,4,256]{3,2,1,0:T(4,128)S(1)} %slice.122), kind=kLoop, calls=%fused_computation.2 | loop fusion | flops 25165824 | bytes 100663296 | tf_op jit(solution)/shard_map/transpose | solution.py:88
  303.3 21.7 %copy.22 = f32[96,64,4,256]{3,2,1,0:T(4,128)} copy(f32[96,64,4,256]{3,2,0,1:T(4,128)} %fusion.1) | data formatting | bytes 50331648 | tf_op jit(solution)/shard_map/transpose | solution.py:88
  325.0 28.8 %reshape.1140 = f32[96,256,256]{2,1,0:T(8,128)} reshape(f32[96,64,4,256]{3,2,1,0:T(4,128)} %copy.22) | data formatting | bytes 50331648 | tf_op jit(solution)/shard_map/reshape | solution.py:88
  354.9 9.9 slice.141
  364.8 9.6 maximum_bitcast_fusion
  374.4 10.0 fusion.187
  387.7 180.0 %collective-permute-done = f32[1,32,256,256]{3,2,1,0:T(8,128)S(1)} collective-permute-done((f32[1,32,256,256]{3,2,1,0:T(8,128)}, f32[1,32,256,256]{3,2,1,0:T(8,128)S(1)}, u32[]{:S(2)}, u32[]{:S(2)}) %collective-permute-start) | collective-permute-done | bytes 8388640 | tf_op jit(solution)/shard_map/ppermute | solution.py:19
  569.9 10.1 fusion.2
  580.0 144.7 %reduce-scatter.2.cloned.1.call-done = f32[1,32,64,256]{3,2,1,0:T(8,128)} async-done(((f32[1,32,256,256]{3,2,1,0:T(8,128)}), f32[1,32,64,256]{3,2,1,0:T(8,128)}) %reduce-scatter.2.cloned.1.call-update) | async-done | bytes 2097168 | tf_op jit(solution)/shard_map/reduce_scatter | solution.py:124
  734.3 9.1 copy.23
  743.5 8.6 reshape.1151
  752.1 99.5 %all_to_all.30 = f32[4,1,262144]{2,1,0:T(1,128)} all-to-all(f32[4,1,262144]{2,1,0:T(1,128)} %reshape.1151), channel_id=1, replica_groups=mesh['slab'=8,'atom'=4] {'atom'}, dimensions={0} | all-to-all | bytes 8388608 | tf_op jit(solution)/shard_map/all_to_all | solution.py:137
  852.1 15.5 %reduce = f32[4,262144]{1,0:T(4,128)} reduce(f32[4,1,262144]{2,1,0:T(1,128)} %all_to_all.30, f32[]{:T(128)} %broadcast.3019), dimensions={1}, to_apply=%all_to_all.22.reduce_sub_computation | reduce | bytes 8388612 | tf_op jit(solution)/shard_map/all_to_all | solution.py:137
  867.6 9.2 reshape.1152
  876.8 12.0 %copy.34 = f32[2,32,64,4,64]{2,3,4,1,0:T(4,128)} copy(f32[2,32,64,4,64]{2,1,0,4,3:T(8,128)} %bitcast.657) | data formatting | bytes 8388608 | tf_op jit(solution)/shard_map/all_to_all | solution.py:137
  888.8 7.8 fusion.189
  923.3 9.1 copy.25
  932.4 9.8 reshape.1153
  952.3 44.1 %all-to-all-done.1 = f32[8,1,131072]{2,1,0:T(1,128)} async-done(((f32[8,1,131072]{2,1,0:T(1,128)}), f32[8,1,131072]{2,1,0:T(1,128)}, u32[]{:S(2)}, u32[]{:S(2)}) %all-to-all-start.1) | async-done | bytes 4194336 | tf_op jit(solution)/shard_map/all_to_all | solution.py:139
  996.4 13.8 %reduce.1 = f32[8,131072]{1,0:T(8,128)} reduce(f32[8,1,131072]{2,1,0:T(1,128)} %all-to-all-done.1, f32[]{:T(128)} %broadcast.3019), dimensions={1}, to_apply=%all_to_all.25.reduce_sub_computation | reduce | bytes 8388612 | tf_op jit(solution)/shard_map/all_to_all | solution.py:139
  1010.2 8.7 reshape.1154
  1018.9 8.2 copy.26
  1068.6 37.8 %psum.7 = f32[7]{0:T(128)S(1)} all-reduce(f32[7]{0:T(128)S(1)} %stack.67), channel_id=1, replica_groups=mesh['slab'=8,'atom'=4] {'slab','atom'}, use_global_device_ids=true, to_apply=%region_8.9 | all-reduce | flops 7 | bytes 56 | tf_op jit(solution)/shard_map/psum | solution.py:182
  (70 shorter events, 109.2 us)
Async XLA Ops:
  7.2 717.5 %reduce-scatter.2.cloned.1.call-start = ((), (), s32[]{:S(2)}) async-start(), calls=%async_computation.3 | async-start | bytes 10485760 | tf_op jit(solution)/shard_map/reduce_scatter | solution.py:124
  75.9 15.8 %copy-start = (f32[64,384,256]{2,1,0:T(8,128)}, f32[64,384,256]{2,1,0:T(8,128)S(1)}, u32[]{:S(2)}) copy-start(f32[64,384,256]{2,1,0:T(8,128)S(1)} %fusion.4) | copy-start | bytes 75497472
  147.1 28.3 %slice-start = ((f32[64,384,256]{2,1,0:T(8,128)}), f32[1,384,256]{2,1,0:T(8,128)S(1)}, s32[]{:S(2)}) async-start(f32[64,384,256]{2,1,0:T(8,128)} %copy-done), calls=%async_computation.4 | async-start | bytes 786432 | tf_op jit(solution)/shard_map/jit(_roll_static)/slice | solution.py:87
  384.3 183.3 %collective-permute-start = (f32[1,32,256,256]{3,2,1,0:T(8,128)}, f32[1,32,256,256]{3,2,1,0:T(8,128)S(1)}, u32[]{:S(2)}, u32[]{:S(2)}) collective-permute-start(f32[1,32,256,256]{3,2,1,0:T(8,128)} %get-tuple-element.13), channel_id=1, source_target_pairs={{0,28},{4,0},{8,4},{12,8},{16,12},{20,16},{24,20},{28,24},{1,29},{... | collective-permute-start | bytes 25165832 | tf_op jit(solution)/shard_map/ppermute | solution.py:19
  387.7 182.2 %collective-permute-start.1 = (f32[1,32,256,256]{3,2,1,0:T(8,128)S(1)}, f32[1,32,256,256]{3,2,1,0:T(8,128)}, u32[]{:S(2)}, u32[]{:S(2)}) collective-permute-start(f32[1,32,256,256]{3,2,1,0:T(8,128)S(1)} %get-tuple-element.14), channel_id=1, source_target_pairs={{0,4},{4,8},{8,12},{12,16},{16,20},{20,24},{24,28},{28,0},{1,5},{5... | collective-permute-start | bytes 25165832 | tf_op jit(solution)/shard_map/ppermute | solution.py:19
  724.7 4.5 copy-start.3
  913.8 5.8 copy-start.4
  913.8 5.8 copy-start.5
  942.2 5.1 copy-start.7
  942.2 54.2 %all-to-all-start.1 = ((f32[8,1,131072]{2,1,0:T(1,128)}), f32[8,1,131072]{2,1,0:T(1,128)}, u32[]{:S(2)}, u32[]{:S(2)}) async-start(f32[8,1,131072]{2,1,0:T(1,128)} %reshape.1153), calls=%async_computation.2 | async-start | bytes 8388608 | tf_op jit(solution)/shard_map/all_to_all | solution.py:139
  1036.6 4.1 copy-start.1
  1052.4 2.9 copy-start.2
  1052.4 2.9 copy-start.6
Sparse Core Ops, SparseCore 0:
  580.1 144.4 reduce-scatter.1
where the time goes:
time: 1130 us; the launch traced here: 1120 us
  waiting for transfers between devices  371 us (33%)
  local copies, waits for them, and re-layouts  295 us (26%)
  matrix products  171 us (15%)
  blocking collectives  137 us (12%)
  other arithmetic  119 us (11%)
  between operations  16.4 us (1%)
    ppermute x2, waiting for transfers between devices, from_behind(): return lax.ppermute(x, axis, [(i, (i + by) % count) for i in range(count)])  182 us
    reduce_scatter x1, waiting for transfers between devices, reduce_shards(): return lax.psum_scatter(data, 'atom', scatter_dimension=2, tiled=True)  145 us
    dot_general x3, matrix products, spread(): product = jnp.einsum('tsa,tsx->tax', left, table_x, precision=highest)  133 us
    all_to_all x1, blocking collectives, body(): data = lax.all_to_all(data, 'atom', split_axis=3, concat_axis=2, tiled=True)  99.5 us
    slice x9, local copies, waits for them, and re-layouts, spread(): summed = summed + jnp.roll(product, shift_by, axis=0)  75.8 us
    all_to_all x1, waiting for transfers between devices, body(): data = lax.all_to_all(data, 'slab', split_axis=2, concat_axis=1, tiled=True)  44.1 us
    unnamed x20, local copies, waits for them, and re-layouts  41.8 us
    psum x1, blocking collectives, body(): totals = lax.psum(local_terms, ('slab', 'atom')) / count  37.8 us
  transfers between devices with their start and end apart: 4, of which 4 were waited for; matrix products, arithmetic and copies ran while one was open for 0% of the time, Pallas kernels for 0%

commit v1 on v0

v1 whole, which is shorter than its diff:
```python
import functools
import math

import jax
import jax.numpy as jnp
import numpy as np
from jax import lax
from jax.experimental import pallas as pl
from jax.experimental.pallas import tpu as pltpu
from jax.sharding import PartitionSpec as P

K = 256
TILES = 64
ORDER = 6
BELOW = 2
ABOVE = 3
HALO = BELOW + ABOVE

ewald_beta = 1.25
f32 = jnp.float32
bf16 = jnp.bfloat16


def split_const(table):
    high = np.asarray(table, np.float32).astype(jnp.bfloat16)
    low = (np.asarray(table, np.float64) - high.astype(np.float64)).astype(np.float32)
    return high, low.astype(jnp.bfloat16)


def dft_const():
    index = np.arange(K)
    angle = 2.0 * np.pi * (np.outer(index, index) % K) / K
    return np.cos(angle), np.sin(angle)


def moduli_const():
    angle = 2.0 * np.pi * np.arange(K) / K
    denom = 66.0 + 52.0 * np.cos(angle) + 2.0 * np.cos(2.0 * angle)
    return ((120.0 / denom) ** 2).astype(np.float32)


def split(x):
    high = x.astype(bf16)
    low = (x - high.astype(f32)).astype(bf16)
    return high, low


def dot(a, b):
    return lax.dot_general(a, b, (((1,), (0,)), ((), ())), preferred_element_type=f32)


def dot_nt(a, b):
    return lax.dot_general(a, b, (((1,), (1,)), ((), ())), preferred_element_type=f32)


def spline_taps(frac):
    prior = [jnp.ones_like(frac)]
    for order in range(2, ORDER + 1):
        scale = 1.0 / (order - 1)
        nxt = []
        for i in range(order):
            terms = []
            if i < order - 1:
                terms.append(((frac + i) * scale) * prior[i])
            if i > 0:
                terms.append(((order - i) - frac) * scale * prior[i - 1])
            nxt.append(terms[0] if len(terms) == 1 else terms[0] + terms[1])
        prior = nxt
    return prior


def iota(shape, dim):
    return lax.broadcasted_iota(jnp.int32, shape, dim)


def spread_kernel(
    counts, where_x, atoms, table_x, high_y, low_y, out, left, right, packed, *, shards, tiles, slots, depth, rows_tile
):
    planes = depth + HALO
    stride = -(-planes // 8) * 8
    window = rows_tile + HALO
    fields = 7 * tiles + 8
    group = 2 * slots
    quarter = table_x.shape[2] // 2

    left[...] = jnp.zeros_like(left)
    right[...] = jnp.zeros_like(right)

    def tile_step(t, _):
        lanes = iota((1, slots), 1)
        sums = [jnp.zeros((7, slots), f32) for _ in range(shards)]
        offset = jnp.int32(0)
        for j in range(shards):
            count = counts[j, t]
            rows = jnp.concatenate(
                [atoms[pl.ds(j * fields + f * tiles + t, 1), :] for f in range(7)], axis=0
            )
            rolled = pltpu.roll(rows, offset & (slots - 1), 1)
            for g in range(j + 1):
                at = lanes + g * slots
                sums[g] = jnp.where((at >= offset) & (at < offset + count), rolled, sums[g])
            offset = offset + count
        for g in range(shards):
            packed[pl.ds(0, 7), pl.ds(g * slots, slots)] = sums[g]

        def group_step(k, _):
            part = packed[:, pl.ds(pl.multiple_of(k * group, group), group)]
            taps = spline_taps(part)
            cell = part.astype(jnp.int32)
            weight = part[6:7]

            def row_of(i, r):
                return taps[i][r : r + 1]

            from_z = iota((stride, group), 0) - (cell[0:1] & (depth - 1))
            along_z = jnp.zeros((stride, group), f32)
            from_y = iota((16, group), 0) - (cell[1:2] & (rows_tile - 1))
            along_y = jnp.zeros((16, group), f32)
            start = (cell[2:3] - BELOW) & (K - 1)
            lane_s = iota((8, group), 0)
            within = start & 7
            turn = (lane_s - within) & 7
            block = ((start >> 3) + jnp.where(lane_s < within, 1, 0)) & (K // 8 - 1)
            along_x = jnp.zeros((8, group), f32)
            for i in range(ORDER):
                hit = ORDER - 1 - i
                along_z = jnp.where(from_z == hit, row_of(i, 3) * weight, along_z)
                along_y = jnp.where(from_y == hit, row_of(i, 4), along_y)
                along_x = jnp.where(turn == hit, row_of(i, 5), along_x)
            x_high = along_x.astype(bf16).astype(f32)
            x_low = along_x - x_high
            highs, lows = [], []
            for b in range(K // 8):
                mask = block == b
                highs.append(jnp.where(mask, x_high, 0.0))
                lows.append(jnp.where(mask, x_low, 0.0))
            t_high = jnp.concatenate(highs, axis=0).astype(bf16)
            t_low = jnp.concatenate(lows, axis=0).astype(bf16)
            outer = jnp.concatenate(
                [along_z * along_y[q : q + 1] for q in range(window)]
                + [jnp.zeros((8, group), f32)] * (window * stride % 16 // 8),
                axis=0,
            )
            o_high, o_low = split(outer)
            result = dot_nt(o_high, t_high) + dot_nt(o_high, t_low) + dot_nt(o_low, t_high)
            at = pl.ds(pl.multiple_of(t * (rows_tile * stride), 8), window * stride)
            left[at, :] += result[: window * stride, : K // 2]
            right[at, :] += result[: window * stride, K // 2 :]
            return 0

        lax.fori_loop(0, (offset + group - 1) // group, group_step, 0)
        return 0

    packed[...] = jnp.zeros_like(packed)
    lax.fori_loop(0, tiles, tile_step, 0)
    for ref in (left, right):
        ref[pl.ds(K * stride, BELOW * stride), :] += ref[pl.ds(0, BELOW * stride), :]
        ref[pl.ds(BELOW * stride, ABOVE * stride), :] += ref[pl.ds((K + BELOW) * stride, ABOVE * stride), :]

    sign = jnp.where(iota((1, 2 * (quarter // 2)), 1) < quarter // 2, 1.0, -1.0)

    def plane_step(p, _):
        at = pl.ds(BELOW * stride + p, K, stride=stride)
        plane = jnp.concatenate([left[at, :], right[at, :]], axis=1)
        high, low = split(plane)
        tab = table_x[where_x[0]]
        first = dot(high, tab)
        in_x = first[:, :quarter] + first[:, quarter:] + dot(low, tab[:, :quarter])
        xh, xl = split(in_x)
        second = dot(high_y[...], jnp.concatenate([xh, xl], axis=1))
        in_y = second[:, :quarter] + second[:, quarter:] + dot(low_y[...], xh)
        by_cos, by_sin = in_y[:K], in_y[K:]
        done = by_cos + pltpu.roll(by_sin, quarter // 2, 1) * sign
        slot = jnp.where(p < BELOW, p + ABOVE + depth, p + ABOVE - BELOW)
        slot = jnp.where(p < BELOW + depth, slot, p - BELOW - depth)
        out[pl.ds(slot, K, stride=planes), :] = done
        return 0

    lax.fori_loop(0, planes, plane_step, 0)


def final_kernel(
    where_k, box, data, table_high, table_low, mod_row, mod_col, field, sums, m_y, g_y, acc, *, slabs, depth, quarter, n_dev, norm
):
    planes = depth + HALO
    pair = 2
    scale = math.pi**2 / ewald_beta**2

    def folded(index):
        return jnp.where(index < K // 2, index, index - K).astype(f32)

    row_z = folded(iota((1, K), 1)) / box[0]
    col_x = folded(iota((quarter, 1), 0) + where_k[1] * quarter) / box[2]
    rows_y = folded(iota((depth, K), 0) + where_k[0] * depth) / box[1]
    mod_x = mod_col[pl.ds(pl.multiple_of(where_k[1] * quarter, 8), quarter), :]
    mod_y = mod_col[pl.ds(pl.multiple_of(where_k[0] * depth, 8), depth), :]
    m_y[...] = rows_y
    g_y[...] = jnp.exp(-scale * rows_y * rows_y) * mod_y
    volume = box[0] * box[1] * box[2]
    base_zx = jnp.exp(-scale * row_z * row_z) * mod_row[...] * (
        jnp.exp(-scale * col_x * col_x) * mod_x / (math.pi * volume)
    )
    sq_zx = row_z * row_z + col_x * col_x
    acc[...] = jnp.zeros_like(acc)
    ids = iota((8, 2 * quarter), 0)

    def step(k, _):
        tr = []
        for u in range(pair):
            ky = k * pair + u
            blocks = []
            for s in range(slabs):
                here = (s * depth + ky) * planes
                before = (((s - 1) % slabs) * depth + ky) * planes
                after = (((s + 1) % slabs) * depth + ky) * planes
                first = data[pl.ds(here + ABOVE, 8), :] + jnp.where(
                    ids < ABOVE, data[pl.ds(before, 8), :], 0.0
                )
                mid = data[pl.ds(here + ABOVE + 8, depth - 16), :]
                last = data[pl.ds(here + ABOVE + depth - 8, 8), :] + jnp.where(
                    ids >= 8 - BELOW, data[pl.ds(after + planes - 8, 8), :], 0.0
                )
                blocks += [first, mid, last]
            tr.append(jnp.concatenate(blocks, axis=0).T)
        high, low = split(jnp.concatenate(tr, axis=0))
        both = dot(high, table_high[...]) + dot(high, table_low[...]) + dot(low, table_high[...])
        for u in range(pair):
            ky = k * pair + u
            lo, mi, hi = (2 * u * quarter, (2 * u + 1) * quarter, (2 * u + 2) * quarter)
            real = both[lo:mi, :K] + both[mi:hi, K:]
            imag = both[mi:hi, :K] - both[lo:mi, K:]
            my = m_y[pl.ds(ky, 1), :]
            msq = sq_zx + my * my
            anchor = msq == 0.0
            inverse = 1.0 / jnp.where(anchor, 1.0, msq)
            theta = jnp.where(anchor, 0.0, base_zx * g_y[pl.ds(ky, 1), :] * inverse)
            fr = theta * real
            fi = theta * imag
            field[0, ky] = fr
            field[1, ky] = fi
            half = 0.5 * (fr * real + fi * imag)
            g = half * (2.0 * inverse + 2.0 * scale)
            gy = g * my
            acc[0] += half
            acc[1] += g
            acc[2] += gy
            acc[3] += gy * my
        return 0

    lax.fori_loop(0, depth // pair, step, 0)

    def total(x):
        return jnp.sum(jnp.sum(x, axis=0, keepdims=True), axis=1, keepdims=True)

    energy = total(acc[0])
    g, gy = acc[1], acc[2]
    values = [
        energy,
        energy - total(g * row_z * row_z),
        energy - total(acc[3]),
        energy - total(g * col_x * col_x),
        -total(gy * row_z),
        -total(g * row_z * col_x),
        -total(gy * col_x),
    ]
    lane = iota((n_dev, 128), 1)
    line = jnp.zeros((n_dev, 128), f32)
    for i, value in enumerate(values):
        line = jnp.where(lane == i, value * norm, line)
    sums[...] = line


def vmem():
    return pl.BlockSpec(memory_space=pltpu.VMEM)


def smem():
    return pl.BlockSpec(memory_space=pltpu.SMEM)


def body(cells, fractions, charges, counts, box):
    slabs = lax.axis_size("slab")
    shards = lax.axis_size("atom")
    tiles, slots = charges.shape
    depth = K // slabs
    quarter = K // shards
    rows_tile = K // tiles
    planes = depth + HALO
    stride = -(-planes // 8) * 8
    n_dev = slabs * shards
    norm = 1.0 / (tiles * slabs * slots * shards)
    a = lax.axis_index("atom").astype(jnp.int32)
    s = lax.axis_index("slab").astype(jnp.int32)

    live = (jnp.arange(slots, dtype=jnp.int32)[None, :] < counts).astype(f32)
    mine = jnp.concatenate(
        [
            cells.astype(f32).reshape(3 * tiles, slots),
            fractions.reshape(3 * tiles, slots),
            charges * live,
            jnp.broadcast_to(jnp.pad(counts[:, 0].astype(f32), (0, slots - tiles))[None], (8, slots)),
        ]
    )
    gathered = lax.all_gather(mine, "atom", axis=0)
    all_counts = gathered[:, 7 * tiles, :tiles].astype(jnp.int32)

    cosine, sine = dft_const()
    per_x = []
    for i in range(shards):
        part = slice(i * quarter, (i + 1) * quarter)
        high, low = split_const(np.concatenate([cosine[:, part], -sine[:, part]], axis=1))
        per_x.append(np.concatenate([high, low], axis=1))
    table_x = jnp.asarray(np.stack(per_x))
    high_y, low_y = split_const(np.concatenate([cosine, sine], axis=0))
    high_z, low_z = split_const(np.concatenate([cosine, sine], axis=1))

    fields = 7 * tiles + 8
    spectrum = pl.pallas_call(
        functools.partial(
            spread_kernel, shards=shards, tiles=tiles, slots=slots, depth=depth, rows_tile=rows_tile
        ),
        out_shape=jax.ShapeDtypeStruct((K * planes, 2 * quarter), f32),
        in_specs=[smem(), smem(), vmem(), vmem(), vmem(), vmem()],
        out_specs=vmem(),
        scratch_shapes=[
            pltpu.VMEM(((K + HALO) * stride, K // 2), f32),
            pltpu.VMEM(((K + HALO) * stride, K // 2), f32),
            pltpu.VMEM((8, shards * slots), f32),
        ],
        compiler_params=pltpu.CompilerParams(vmem_limit_bytes=60 * 1024 * 1024),
        name="spread",
    )(
        all_counts,
        a[None],
        gathered.reshape(shards * fields, slots),
        table_x,
        jnp.asarray(high_y),
        jnp.asarray(low_y),
    )
    moved = lax.all_to_all(
        spectrum.reshape(slabs, depth * planes, 2 * quarter), "slab", 0, 0, tiled=True
    )
    mod = moduli_const()
    if depth % 16:
        return plain_final(moved, box, high_z, a, s, slabs, depth, quarter, norm)
    field, sums = pl.pallas_call(
        functools.partial(
            final_kernel, slabs=slabs, depth=depth, quarter=quarter, n_dev=n_dev, norm=norm
        ),
        out_shape=(
            jax.ShapeDtypeStruct((2, depth, quarter, K), f32),
            jax.ShapeDtypeStruct((n_dev, 128), f32),
        ),
        in_specs=[smem(), smem(), vmem(), vmem(), vmem(), vmem(), vmem()],
        out_specs=(vmem(), vmem()),
        scratch_shapes=[
            pltpu.VMEM((depth, K), f32),
            pltpu.VMEM((depth, K), f32),
            pltpu.VMEM((4, quarter, K), f32),
        ],
        compiler_params=pltpu.CompilerParams(vmem_limit_bytes=60 * 1024 * 1024),
        name="final",
    )(
        jnp.stack([s, a]),
        box,
        moved.reshape(K * planes, 2 * quarter),
        jnp.asarray(high_z),
        jnp.asarray(low_z),
        jnp.asarray(mod[None, :]),
        jnp.asarray(mod[:, None]),
    )
    return field, spread_totals(sums)


def spread_totals(sums):
    shared = lax.all_to_all(sums, ("slab", "atom"), 0, 0, tiled=True)
    return jnp.sum(shared[:, :7], axis=0)


def plain_final(moved, box, table, a, s, slabs, depth, quarter, norm):
    planes = depth + HALO
    highest = lax.Precision.HIGHEST
    data = moved.reshape(slabs, depth, planes, 2 * quarter)
    own = data[:, :, ABOVE : ABOVE + depth]
    up = jnp.roll(data[:, :, :ABOVE], 1, axis=0)
    down = jnp.roll(data[:, :, ABOVE + depth :], -1, axis=0)
    own = own.at[:, :, :ABOVE].add(up).at[:, :, depth - BELOW :].add(down)
    cosine, sine = (jnp.asarray(t.astype(np.float32)) for t in dft_const())
    flat = jnp.transpose(own, (1, 3, 0, 2)).reshape(depth, 2 * quarter, K)
    real_in, imag_in = flat[:, :quarter], flat[:, quarter:]
    times = functools.partial(jnp.einsum, "yxz,zk->yxk", precision=highest)
    real_part = times(real_in, cosine) + times(imag_in, sine)
    imag_part = times(imag_in, cosine) - times(real_in, sine)
    index_z = jnp.arange(K, dtype=jnp.int32)
    index_y = s * depth + jnp.arange(depth, dtype=jnp.int32)
    index_x = a * quarter + jnp.arange(quarter, dtype=jnp.int32)
    mod = jnp.asarray(moduli_const())

    def folded(index):
        return jnp.where(index < K // 2, index, index - K).astype(f32)

    m_z = (folded(index_z) / box[0])[None, None, :]
    m_y = (folded(index_y) / box[1])[:, None, None]
    m_x = (folded(index_x) / box[2])[None, :, None]
    msq = m_z * m_z + m_y * m_y + m_x * m_x
    anchor = msq == 0.0
    safe = jnp.where(anchor, 1.0, msq)
    volume = box[0] * box[1] * box[2]
    spline_part = mod[index_z][None, None, :] * mod[index_y][:, None, None] * mod[index_x][None, :, None]
    theta = jnp.exp(-math.pi**2 * safe / ewald_beta**2) * spline_part / (math.pi * volume * safe)
    theta = jnp.where(anchor, 0.0, theta)
    half = 0.5 * theta * (real_part * real_part + imag_part * imag_part)
    factor = 2.0 * (1.0 + math.pi**2 * safe / ewald_beta**2) / safe
    terms = [
        half,
        half * (1.0 - factor * m_z * m_z),
        half * (1.0 - factor * m_y * m_y),
        half * (1.0 - factor * m_x * m_x),
        half * (-factor * m_z * m_y),
        half * (-factor * m_z * m_x),
        half * (-factor * m_y * m_x),
    ]
    totals = lax.psum(jnp.stack([jnp.sum(term) for term in terms]), ("slab", "atom")) * norm
    return jnp.stack([theta * real_part, theta * imag_part]), totals


def solution(mesh):
    in_specs = (
        P(None, "slab", "atom"),
        P(None, "slab", "atom"),
        P("slab", "atom"),
        P("slab", "atom"),
        P(),
    )
    out_specs = (P(None, "slab", "atom", None), P())
    return jax.shard_map(body, mesh=mesh, in_specs=in_specs, out_specs=out_specs, check_vma=False)
```

time: 1130 us -> 181 us (0.16); the launches traced: 1120 us -> 181 us
  waiting for transfers between devices: 371 us -> 55.6 us
  local copies, waits for them, and re-layouts: 295 us -> 0.32 us
  matrix products: 171 us -> 0 us
  other arithmetic: 119 us -> 5.01 us
  blocking collectives: 137 us -> 32.6 us
  Pallas kernels: 0 us -> 82.7 us
  between operations: 16.4 us -> 0.67 us
    ppermute x2 -> x0, waiting for transfers between devices: 182 us -> none  [from_behind(): return lax.ppermute(x, axis, [(i, (i + by) % count) for i in range(count)])]
    dot_general x9 -> x0, matrix products: 157 us -> none  [the longest x3 133 us: spread(): product = jnp.einsum('tsa,tsx->tax', left, table_x, precision=highest)]
    reduce_scatter x1 -> x0, waiting for transfers between devices: 145 us -> none  [reduce_shards(): return lax.psum_scatter(data, 'atom', scatter_dimension=2, tiled=True)]
    slice x18 -> x1, local copies, waits for them, and re-layouts: 114 us -> 0.01 us  [body(): all_counts = gathered[:, 7 * tiles, :tiles].astype(jnp.int32)]
    all_to_all x1, blocking collectives: 99.5 us -> 9.66 us  [spread_totals(): shared = lax.all_to_all(sums, ('slab', 'atom'), 0, 0, tiled=True)]
    pallas_call x0 -> x2, Pallas kernels: none -> 82.7 us  [the longest x1 70.6 us: body(): pl.pallas_call(functools.partial(spread_kernel, shards=shards, tiles=tile...]
    reshape x2 -> x0, local copies, waits for them, and re-layouts: 57 us -> none  [the longest x1 28.8 us: spread(): jnp.transpose(summed, (1, 0, 2, 3)).reshape(planes, tiles * rows_tile, K)]
    unnamed x20 -> x2, local copies, waits for them, and re-layouts: 41.8 us -> 0.31 us
  transfers between devices with their start and end apart: 4 -> 1, of which waited for: 4 -> 1; matrix products, arithmetic and copies ran while one was open for 0% -> 0% of each run, Pallas kernels for 0% -> 0%
where the time goes in v1:
time: 181 us
  Pallas kernels  82.7 us (46%)
  waiting for transfers between devices  55.6 us (31%)
  blocking collectives  32.6 us (18%)
  other arithmetic  5.01 us (3%)
  starting transfers between devices  4.6 us (3%)
    pallas_call x1, Pallas kernels, body(): pl.pallas_call(functools.partial(spread_kernel, shards=shards, tiles=tile...  70.6 us
    all_to_all x1, waiting for transfers between devices, body(): lax.all_to_all(spectrum.reshape(slabs, depth * planes, 2 * quarter), 'sla...  55.6 us
    all_gather x1, blocking collectives, body(): gathered = lax.all_gather(mine, 'atom', axis=0)  22.9 us
    pallas_call x1, Pallas kernels, body(): pl.pallas_call(functools.partial(final_kernel, slabs=slabs, depth=depth,...  12.1 us
    all_to_all x1, blocking collectives, spread_totals(): shared = lax.all_to_all(sums, ('slab', 'atom'), 0, 0, tiled=True)  9.66 us
    all_to_all x1, starting transfers between devices, body(): lax.all_to_all(spectrum.reshape(slabs, depth * planes, 2 * quarter), 'sla...  4.6 us
  transfers between devices with their start and end apart: 1, of which 1 were waited for; matrix products, arithmetic and copies ran while one was open for 0% of the time, Pallas kernels for 0%

profile of v1, /device:TPU:0, one launch (start us, length us, event | category | flops | bytes accessed | tf_op | source)
XLA Modules:
  0.0 181.4 jit_solution(1288095316876658925)
XLA Ops:
  0.6 0.7 bitcast_convert_fusion
  1.3 0.9 convert_element_type.14
  2.2 0.8 fusion
  3.0 0.9 pad_maximum_fusion
  4.0 22.9 %all-gather.atoms = f32[1824,128]{1,0:T(8,128)S(1)} all-gather(f32[456,128]{1,0:T(8,128)S(1)} %pad_maximum_fusion), channel_id=2, replica_groups=mesh['slab'=8,'atom'=4] {'atom'}, dimensions={0}, use_global_device_ids=true | all-gather | bytes 1167360 | tf_op jit(solution)/shard_map/all_gather | solution.py:304
  26.9 0.0 copy-start
  26.9 0.6 convert_bitcast_fusion.counts
  27.5 0.3 copy-done
  27.8 70.6 %spread.1 = f32[9472,128]{1,0:T(8,128)} custom-call(s32[4,64]{1,0:T(4,128)} %convert_bitcast_fusion.counts, s32[1]{0:T(128)} %bitcast.1.where_x, f32[1824,128]{1,0:T(8,128)} %copy-done, bf16[4,256,256]{2,1,0:T(8,128)(2,1)} %constant.28.clone.table_x, bf16[512,256]{1,0:T(8,128)(2,1)} %constant.29.clone.high_y, bf16[512,256]{1,0:T(8,128)(2,1)} %constant.30.clone.low_y), custom_call_target="tpu_custom_call" | custom-call | tf_op jit(solution)/shard_map/spread/pallas_call | solution.py:318
  98.4 4.6 %all-to-all-start = ((f32[8,1184,128]{2,1,0:T(8,128)}), f32[8,1184,128]{2,1,0:T(8,128)}, u32[]{:S(2)}, u32[]{:S(2)}) async-start(f32[8,1184,128]{2,1,0:T(8,128)} %bitcast.16), calls=%async_computation | async-start | bytes 9699328 | tf_op jit(solution)/shard_map/all_to_all | solution.py:340
  103.0 0.6 pad_add_fusion.where_k
  103.6 55.6 %all-to-all-done = f32[8,1184,128]{2,1,0:T(8,128)} async-done(((f32[8,1184,128]{2,1,0:T(8,128)}), f32[8,1184,128]{2,1,0:T(8,128)}, u32[]{:S(2)}, u32[]{:S(2)}) %all-to-all-start) | async-done | bytes 4849696 | tf_op jit(solution)/shard_map/all_to_all | solution.py:340
  159.1 12.1 %final.1 = (f32[2,32,64,256]{3,2,1,0:T(8,128)}, f32[32,128]{1,0:T(8,128)}) custom-call(s32[2]{0:T(128)} %pad_add_fusion.where_k, f32[3]{0:T(128)} %box.1, f32[9472,128]{1,0:T(8,128)} %bitcast.8.data, bf16[256,512]{1,0:T(8,128)(2,1)} %constant.31.clone.table_high, bf16[256,512]{1,0:T(8,128)(2,1)} %constant.32.clone.table_low, ...), custom_call_target="tpu_custom_call" | custom-call | tf_op jit(solution)/shard_map/final/pallas_call | solution.py:346
  171.2 9.7 %all_to_all.17 = f32[32,1,128]{2,1,0:T(1,128)S(1)} all-to-all(f32[32,1,128]{2,1,0:T(1,128)} %bitcast.21), channel_id=1, replica_groups=mesh['slab'=8,'atom'=4] {'slab','atom'}, dimensions={0} | all-to-all | bytes 32768 | tf_op jit(solution)/shard_map/all_to_all | solution.py:376
  180.9 0.5 slice_reduce_fusion
  (3 shorter events, 0.0 us)
Async XLA Ops:
  26.9 0.9 copy-start
  98.4 60.7 %all-to-all-start = ((f32[8,1184,128]{2,1,0:T(8,128)}), f32[8,1184,128]{2,1,0:T(8,128)}, u32[]{:S(2)}, u32[]{:S(2)}) async-start(f32[8,1184,128]{2,1,0:T(8,128)} %bitcast.16), calls=%async_computation | async-start | bytes 9699328 | tf_op jit(solution)/shard_map/all_to_all | solution.py:340

commit v2 on v1

v2 whole, which is shorter than its diff:
```python
import functools
import math

import jax
import jax.numpy as jnp
import numpy as np
from jax import lax
from jax.experimental import pallas as pl
from jax.experimental.pallas import tpu as pltpu
from jax.sharding import PartitionSpec as P

K = 256
TILES = 64
ORDER = 6
BELOW = 2
ABOVE = 3
HALO = BELOW + ABOVE

ewald_beta = 1.25
f32 = jnp.float32
bf16 = jnp.bfloat16


def split_const(table):
    high = np.asarray(table, np.float32).astype(jnp.bfloat16)
    low = (np.asarray(table, np.float64) - high.astype(np.float64)).astype(np.float32)
    return high, low.astype(jnp.bfloat16)


def dft_const():
    index = np.arange(K)
    angle = 2.0 * np.pi * (np.outer(index, index) % K) / K
    return np.cos(angle), np.sin(angle)


def moduli_const():
    angle = 2.0 * np.pi * np.arange(K) / K
    denom = 66.0 + 52.0 * np.cos(angle) + 2.0 * np.cos(2.0 * angle)
    return ((120.0 / denom) ** 2).astype(np.float32)


def split(x):
    high = x.astype(bf16)
    low = (x - high.astype(f32)).astype(bf16)
    return high, low


def dot(a, b):
    return lax.dot_general(a, b, (((1,), (0,)), ((), ())), preferred_element_type=f32)


def dot_nt(a, b):
    return lax.dot_general(a, b, (((1,), (1,)), ((), ())), preferred_element_type=f32)


def spline_taps(frac):
    ups = [frac] + [frac + float(i) for i in range(1, ORDER - 1)]
    downs = [None] + [float(i) - frac for i in range(1, ORDER)]
    prior = [jnp.ones_like(frac)]
    for order in range(2, ORDER + 1):
        nxt = []
        for i in range(order):
            if i == 0:
                nxt.append(ups[0] * prior[0])
            elif i == order - 1:
                nxt.append(downs[1] * prior[i - 1])
            else:
                nxt.append(ups[i] * prior[i] + downs[order - i] * prior[i - 1])
        prior = nxt
    return prior


def iota(shape, dim):
    return lax.broadcasted_iota(jnp.int32, shape, dim)


def join_kernel(cells, fractions, charges, counts, out, *, tiles):
    out[pl.ds(0, 3 * tiles), :] = cells[...].astype(f32)
    out[pl.ds(3 * tiles, 3 * tiles), :] = fractions[...]
    out[pl.ds(6 * tiles, tiles), :] = charges[...]
    out[pl.ds(7 * tiles, 8), :] = jnp.zeros((8, out.shape[1]), f32)
    out[pl.ds(7 * tiles, 1), pl.ds(0, tiles)] = counts[...].astype(f32)


def pack_tiles(counts, atoms, packed, items, clear, *, shards, tiles, slots):
    fields = 7 * tiles + 8
    most = shards // 2
    lanes = iota((1, slots), 1)
    zero = jnp.zeros((7, slots), f32)

    def step(t, n):
        clear(t)
        sums = [zero] * shards
        offset = jnp.int32(0)
        for j in range(shards):
            count = counts[j, t]
            rows = atoms[pl.ds(j * fields + t, 7, stride=tiles), :]
            rolled = pltpu.roll(rows, offset & (slots - 1), 1)
            for g in range(j + 1):
                at = lanes + g * slots
                sums[g] = jnp.where((at >= offset) & (at < offset + count), rolled, sums[g])
            offset = offset + count
        for g in range(most):
            both = jnp.concatenate([sums[2 * g], sums[2 * g + 1]], axis=1)
            packed[pl.ds(pl.multiple_of((t * most + g) * 8, 8), 8), :] = jnp.concatenate(
                [both, jnp.zeros((1, 2 * slots), f32)], axis=0
            )
            items[n + g] = t * most + g
        return n + (offset + 2 * slots - 1) // (2 * slots)

    n = lax.fori_loop(0, tiles, step, jnp.int32(0))
    packed[pl.ds(tiles * most * 8, 8), :] = jnp.zeros((8, 2 * slots), f32)
    for g in range(2):
        items[n + g] = tiles * most
    return n


def build_tables(part, left_table, right_table, *, stride, window, depth, rows_tile, group):
    taps = spline_taps(part)
    cell = part.astype(jnp.int32)
    weight = part[6:7] * (1.0 / math.factorial(ORDER - 1) ** 3)

    def row_of(i, r):
        return taps[i][r : r + 1]

    start_z = cell[0:1] & (depth - 1)
    start_x = (cell[2:3] - BELOW) & (K - 1)
    id_z, id_x = iota((8, group), 0), iota((16, group), 0)
    within_z, within_x = start_z & 7, start_x & 15
    turn_z, turn_x = (id_z - within_z) & 7, (id_x - within_x) & 15
    block_z = (start_z >> 3) + jnp.where(id_z < within_z, 1, 0)
    block_x = ((start_x >> 4) + jnp.where(id_x < within_x, 1, 0)) & (K // 16 - 1)
    from_y = iota((16, group), 0) - (cell[1:2] & (rows_tile - 1))
    some_z = jnp.zeros((8, group), f32)
    some_x = jnp.zeros((16, group), f32)
    along_y = jnp.zeros((16, group), f32)
    for i in range(ORDER):
        hit = ORDER - 1 - i
        some_z = jnp.where(turn_z == hit, row_of(i, 3) * weight, some_z)
        along_y = jnp.where(from_y == hit, row_of(i, 4), along_y)
        some_x = jnp.where(turn_x == hit, row_of(i, 5), some_x)
    along_z = jnp.concatenate([jnp.where(block_z == b, some_z, 0.0) for b in range(stride // 8)], axis=0)
    x_high, x_low = split(some_x)
    block = block_x.astype(f32).astype(bf16)
    none = jnp.zeros((16, group), bf16)
    for b in range(K // 16):
        mask = block == jnp.asarray(b, bf16)
        right_table[pl.ds(b * 16, 16), pl.ds(0, group)] = jnp.where(mask, x_high, none)
        right_table[pl.ds(b * 16, 16), pl.ds(group, group)] = jnp.where(mask, x_low, none)
    for q in range(0, window, 2):
        rows = [along_z * along_y[u : u + 1] for u in range(q, min(q + 2, window))]
        height = len(rows) * stride
        if height % 16:
            rows.append(jnp.zeros((8, group), f32))
            height += 8
        high, low = split(jnp.concatenate(rows, axis=0))
        left_table[pl.ds(q * stride, height), pl.ds(0, group)] = high
        left_table[pl.ds(q * stride, height), pl.ds(group, group)] = low


def spread_kernel(
    counts,
    where_x,
    atoms,
    table_x,
    high_y,
    low_y,
    out,
    left,
    right,
    packed,
    items,
    lt_a,
    rt_a,
    lt_b,
    rt_b,
    *,
    shards,
    tiles,
    slots,
    depth,
    rows_tile,
):
    planes = depth + HALO
    stride = -(-planes // 8) * 8
    window = rows_tile + HALO
    group = 2 * slots
    most = shards // 2
    half = table_x.shape[2] // 2
    quarter = half // 2
    step_rows = rows_tile * stride

    def clear(t):
        for ref in (left, right):
            ref[pl.ds(pl.multiple_of(t * step_rows, 8), step_rows), :] = jnp.zeros((step_rows, K // 2), f32)

    for ref in (left, right):
        ref[pl.ds(K * stride, HALO * stride), :] = jnp.zeros((HALO * stride, K // 2), f32)
    count = pack_tiles(counts, atoms, packed, items, clear, shards=shards, tiles=tiles, slots=slots)

    def build(i, lt, rt):
        part = packed[pl.ds(pl.multiple_of(items[i] * 8, 8), 8), :]
        build_tables(
            part, lt, rt, stride=stride, window=window, depth=depth, rows_tile=rows_tile, group=group
        )

    def apply(i, lt, rt):
        t = jnp.minimum(items[i] // most, tiles - 1)
        lh, ll = lt[:, :group], lt[:, group:]
        rh, rl = rt[:, :group], rt[:, group:]
        result = dot_nt(
            jnp.concatenate([lh, lh, ll], axis=1), jnp.concatenate([rh, rl, rh], axis=1)
        )
        at = pl.ds(pl.multiple_of(t * step_rows, 8), window * stride)
        left[at, :] += result[: window * stride, : K // 2]
        right[at, :] += result[: window * stride, K // 2 :]

    build(0, lt_a, rt_a)

    def pair_step(j, _):
        apply(2 * j, lt_a, rt_a)
        build(2 * j + 1, lt_b, rt_b)
        apply(2 * j + 1, lt_b, rt_b)
        build(jnp.minimum(2 * j + 2, count), lt_a, rt_a)
        return 0

    lax.fori_loop(0, (count + 1) // 2, pair_step, 0)
    for ref in (left, right):
        ref[pl.ds(K * stride, BELOW * stride), :] += ref[pl.ds(0, BELOW * stride), :]
        ref[pl.ds(BELOW * stride, ABOVE * stride), :] += ref[pl.ds((K + BELOW) * stride, ABOVE * stride), :]

    chunk = 512
    table = table_x[where_x[0]]

    def x_step(c, _):
        at = pl.ds(pl.multiple_of(BELOW * stride + c * chunk, 8), chunk)
        high, low = split(jnp.concatenate([left[at, :], right[at, :]], axis=1))
        upper = dot(high, table)
        lower = dot(low, table[:, :half])
        left[at, :] = (upper[:, :half] + lower) + upper[:, half:]
        return 0

    lax.fori_loop(0, K * stride // chunk, x_step, 0)

    sign = jnp.where(iota((1, half), 1) < quarter, 1.0, -1.0)
    th, tl = high_y[...], low_y[...]

    def slot_of(p):
        slot = jnp.where(p < BELOW, p + ABOVE + depth, p + ABOVE - BELOW)
        return jnp.where(p < BELOW + depth, slot, p - BELOW - depth)

    table_y = jnp.concatenate([th[:K], th[K:], th[:K], th[K:], tl[:K], tl[K:]], axis=1)

    def plane_pair(first):
        at = [first, first + 1]
        data = [left[pl.ds(BELOW * stride + p, K, stride=stride), :] for p in at]
        turned = [pltpu.roll(x, quarter, 1) * sign for x in data]
        high, low = split(jnp.concatenate(data, axis=1))
        high_t, low_t = split(jnp.concatenate(turned, axis=1))
        done = dot(table_y, jnp.concatenate([high, high_t, low, low_t, high, high_t], axis=0))
        for u in range(2):
            out[pl.ds(slot_of(at[u]), K, stride=planes), :] = done[:, u * half : (u + 1) * half]

    def plane_step(j, _):
        for u in range(2):
            plane_pair(jnp.minimum(4 * j + 2 * u, planes - 2))
        return 0

    lax.fori_loop(0, -(-planes // 4), plane_step, 0)


def final_kernel(
    where_k, box, data, table_high, table_low, mod_row, mod_col, field, sums, m_y, g_y, acc, base_zx, sq_zx, *, slabs, depth, quarter, n_dev, norm
):
    planes = depth + HALO
    pair = 4
    here_y = m_y.shape[0]
    g = pl.program_id(0)
    scale = math.pi**2 / ewald_beta**2

    def folded(index):
        return jnp.where(index < K // 2, index, index - K).astype(f32)

    row_z = folded(iota((1, K), 1)) / box[0]
    col_x = folded(iota((quarter, 1), 0) + where_k[1] * quarter) / box[2]

    @pl.when(g == 0)
    def _():
        mod_x = mod_col[pl.ds(pl.multiple_of(where_k[1] * quarter, 8), quarter), :]
        volume = box[0] * box[1] * box[2]
        base_zx[...] = jnp.exp(-scale * row_z * row_z) * mod_row[...] * (
            jnp.exp(-scale * col_x * col_x) * mod_x / (math.pi * volume)
        )
        sq_zx[...] = row_z * row_z + col_x * col_x
        acc[...] = jnp.zeros_like(acc)

    first_y = where_k[0] * depth + g * here_y
    rows_y = folded(iota((here_y, K), 0) + first_y) / box[1]
    m_y[...] = rows_y
    g_y[...] = jnp.exp(-scale * rows_y * rows_y) * mod_col[pl.ds(pl.multiple_of(first_y, 8), here_y), :]
    ids = iota((8, 2 * quarter), 0)

    def step(k, _):
        tr = []
        for u in range(pair):
            row = (k * pair + u) * planes
            blocks = []
            for s in range(slabs):
                first = data[s, pl.ds(row + ABOVE, 8), :] + jnp.where(
                    ids < ABOVE, data[(s - 1) % slabs, pl.ds(row, 8), :], 0.0
                )
                mid = data[s, pl.ds(row + ABOVE + 8, depth - 16), :]
                last = data[s, pl.ds(row + ABOVE + depth - 8, 8), :] + jnp.where(
                    ids >= 8 - BELOW, data[(s + 1) % slabs, pl.ds(row + planes - 8, 8), :], 0.0
                )
                blocks += [first, mid, last]
            tr.append(jnp.concatenate(blocks, axis=0).T)
        high, low = split(jnp.concatenate(tr, axis=0))
        th, tl = table_high[...], table_low[...]
        both = dot(jnp.concatenate([high, high, low], axis=1), jnp.concatenate([th, tl, th], axis=0))
        for u in range(pair):
            ky = k * pair + u
            lo, mi, hi = (2 * u * quarter, (2 * u + 1) * quarter, (2 * u + 2) * quarter)
            real = both[lo:mi, :K] + both[mi:hi, K:]
            imag = both[mi:hi, :K] - both[lo:mi, K:]
            my = m_y[pl.ds(ky, 1), :]
            msq = sq_zx[...] + my * my
            anchor = msq == 0.0
            inverse = 1.0 / jnp.where(anchor, 1.0, msq)
            theta = jnp.where(anchor, 0.0, base_zx[...] * g_y[pl.ds(ky, 1), :] * inverse)
            fr = theta * real
            fi = theta * imag
            field[0, ky] = fr
            field[1, ky] = fi
            half = 0.5 * (fr * real + fi * imag)
            gain = half * (2.0 * inverse + 2.0 * scale)
            gy = gain * my
            acc[0] += half
            acc[1] += gain
            acc[2] += gy
            acc[3] += gy * my
        return 0

    lax.fori_loop(0, here_y // pair, step, 0)

    @pl.when(g == pl.num_programs(0) - 1)
    def _():
        finish(sums, acc, row_z, col_x, n_dev, norm)


def finish(sums, acc, row_z, col_x, n_dev, norm):
    def total(x):
        return jnp.sum(jnp.sum(x, axis=0, keepdims=True), axis=1, keepdims=True)

    energy = total(acc[0])
    g, gy = acc[1], acc[2]
    values = [
        energy,
        energy - total(g * row_z * row_z),
        energy - total(acc[3]),
        energy - total(g * col_x * col_x),
        -total(gy * row_z),
        -total(g * row_z * col_x),
        -total(gy * col_x),
    ]
    lane = iota((n_dev, 128), 1)
    line = jnp.zeros((n_dev, 128), f32)
    for i, value in enumerate(values):
        line = jnp.where(lane == i, value * norm, line)
    sums[...] = line


def vmem():
    return pl.BlockSpec(memory_space=pltpu.VMEM)


def smem():
    return pl.BlockSpec(memory_space=pltpu.SMEM)


def body(cells, fractions, charges, counts, box):
    slabs = lax.axis_size("slab")
    shards = lax.axis_size("atom")
    tiles, slots = charges.shape
    depth = K // slabs
    quarter = K // shards
    rows_tile = K // tiles
    planes = depth + HALO
    stride = -(-planes // 8) * 8
    n_dev = slabs * shards
    norm = 1.0 / (tiles * slabs * slots * shards)
    a = lax.axis_index("atom").astype(jnp.int32)
    s = lax.axis_index("slab").astype(jnp.int32)

    mine = pl.pallas_call(
        functools.partial(join_kernel, tiles=tiles),
        out_shape=jax.ShapeDtypeStruct((7 * tiles + 8, slots), f32),
        in_specs=[vmem()] * 4,
        out_specs=vmem(),
        name="join",
    )(
        cells.reshape(3 * tiles, slots),
        fractions.reshape(3 * tiles, slots),
        charges,
        counts.reshape(1, tiles),
    )
    gathered = lax.all_gather(mine, "atom", axis=0)
    all_counts = gathered[:, 7 * tiles, :tiles].astype(jnp.int32)

    cosine, sine = dft_const()
    per_x = []
    for i in range(shards):
        part = slice(i * quarter, (i + 1) * quarter)
        high, low = split_const(np.concatenate([cosine[:, part], -sine[:, part]], axis=1))
        per_x.append(np.concatenate([high, low], axis=1))
    table_x = jnp.asarray(np.stack(per_x))
    high_y, low_y = split_const(np.concatenate([cosine, sine], axis=0))
    high_z, low_z = split_const(np.concatenate([cosine, sine], axis=1))

    fields = 7 * tiles + 8
    spectrum = pl.pallas_call(
        functools.partial(
            spread_kernel, shards=shards, tiles=tiles, slots=slots, depth=depth, rows_tile=rows_tile
        ),
        out_shape=jax.ShapeDtypeStruct((K * planes, 2 * quarter), f32),
        in_specs=[smem(), smem(), vmem(), vmem(), vmem(), vmem()],
        out_specs=vmem(),
        scratch_shapes=[
            pltpu.VMEM(((K + HALO) * stride, K // 2), f32),
            pltpu.VMEM(((K + HALO) * stride, K // 2), f32),
            pltpu.VMEM((tiles * shards * 4 + 8, 2 * slots), f32),
            pltpu.SMEM((tiles * shards // 2 + shards,), jnp.int32),
        ]
        + [
            pltpu.VMEM((-(-(rows_tile + HALO) * stride // 16) * 16, 4 * slots), bf16),
            pltpu.VMEM((K, 4 * slots), bf16),
        ]
        * 2,
        compiler_params=pltpu.CompilerParams(vmem_limit_bytes=60 * 1024 * 1024),
        name="spread",
    )(
        all_counts,
        a[None],
        gathered.reshape(shards * fields, slots),
        table_x,
        jnp.asarray(high_y),
        jnp.asarray(low_y),
    )
    moved = lax.all_to_all(
        spectrum.reshape(slabs, depth * planes, 2 * quarter), "slab", 0, 0, tiled=True
    )
    mod = moduli_const()
    block_y = 8
    if depth % 16:
        return plain_final(moved, box, high_z, a, s, slabs, depth, quarter, norm)
    field, sums = pl.pallas_call(
        functools.partial(
            final_kernel, slabs=slabs, depth=depth, quarter=quarter, n_dev=n_dev, norm=norm
        ),
        out_shape=(
            jax.ShapeDtypeStruct((2, depth, quarter, K), f32),
            jax.ShapeDtypeStruct((n_dev, 128), f32),
        ),
        grid=(depth // block_y,),
        in_specs=[
            smem(),
            smem(),
            pl.BlockSpec((slabs, block_y * planes, 2 * quarter), lambda g: (0, g, 0)),
            vmem(),
            vmem(),
            vmem(),
            vmem(),
        ],
        out_specs=(
            pl.BlockSpec((2, block_y, quarter, K), lambda g: (0, g, 0, 0)),
            pl.BlockSpec((n_dev, 128), lambda g: (0, 0)),
        ),
        scratch_shapes=[
            pltpu.VMEM((block_y, K), f32),
            pltpu.VMEM((block_y, K), f32),
            pltpu.VMEM((4, quarter, K), f32),
            pltpu.VMEM((quarter, K), f32),
            pltpu.VMEM((quarter, K), f32),
        ],
        compiler_params=pltpu.CompilerParams(vmem_limit_bytes=60 * 1024 * 1024),
        name="final",
    )(
        jnp.stack([s, a]),
        box,
        moved,
        jnp.asarray(high_z),
        jnp.asarray(low_z),
        jnp.asarray(mod[None, :]),
        jnp.asarray(mod[:, None]),
    )
    return field, spread_totals(sums)


def spread_totals(sums):
    shared = lax.all_to_all(sums, ("slab", "atom"), 0, 0, tiled=True)
    return jnp.sum(shared[:, :7], axis=0)


def plain_final(moved, box, table, a, s, slabs, depth, quarter, norm):
    planes = depth + HALO
    highest = lax.Precision.HIGHEST
    data = moved.reshape(slabs, depth, planes, 2 * quarter)
    own = data[:, :, ABOVE : ABOVE + depth]
    up = jnp.roll(data[:, :, :ABOVE], 1, axis=0)
    down = jnp.roll(data[:, :, ABOVE + depth :], -1, axis=0)
    own = own.at[:, :, :ABOVE].add(up).at[:, :, depth - BELOW :].add(down)
    cosine, sine = (jnp.asarray(t.astype(np.float32)) for t in dft_const())
    flat = jnp.transpose(own, (1, 3, 0, 2)).reshape(depth, 2 * quarter, K)
    real_in, imag_in = flat[:, :quarter], flat[:, quarter:]
    times = functools.partial(jnp.einsum, "yxz,zk->yxk", precision=highest)
    real_part = times(real_in, cosine) + times(imag_in, sine)
    imag_part = times(imag_in, cosine) - times(real_in, sine)
    index_z = jnp.arange(K, dtype=jnp.int32)
    index_y = s * depth + jnp.arange(depth, dtype=jnp.int32)
    index_x = a * quarter + jnp.arange(quarter, dtype=jnp.int32)
    mod = jnp.asarray(moduli_const())

    def folded(index):
        return jnp.where(index < K // 2, index, index - K).astype(f32)

    m_z = (folded(index_z) / box[0])[None, None, :]
    m_y = (folded(index_y) / box[1])[:, None, None]
    m_x = (folded(index_x) / box[2])[None, :, None]
    msq = m_z * m_z + m_y * m_y + m_x * m_x
    anchor = msq == 0.0
    safe = jnp.where(anchor, 1.0, msq)
    volume = box[0] * box[1] * box[2]
    spline_part = mod[index_z][None, None, :] * mod[index_y][:, None, None] * mod[index_x][None, :, None]
    theta = jnp.exp(-math.pi**2 * safe / ewald_beta**2) * spline_part / (math.pi * volume * safe)
    theta = jnp.where(anchor, 0.0, theta)
    half = 0.5 * theta * (real_part * real_part + imag_part * imag_part)
    factor = 2.0 * (1.0 + math.pi**2 * safe / ewald_beta**2) / safe
    terms = [
        half,
        half * (1.0 - factor * m_z * m_z),
        half * (1.0 - factor * m_y * m_y),
        half * (1.0 - factor * m_x * m_x),
        half * (-factor * m_z * m_y),
        half * (-factor * m_z * m_x),
        half * (-factor * m_y * m_x),
    ]
    totals = lax.psum(jnp.stack([jnp.sum(term) for term in terms]), ("slab", "atom")) * norm
    return jnp.stack([theta * real_part, theta * imag_part]), totals


def solution(mesh):
    in_specs = (
        P(None, "slab", "atom"),
        P(None, "slab", "atom"),
        P("slab", "atom"),
        P("slab", "atom"),
        P(),
    )
    out_specs = (P(None, "slab", "atom", None), P())
    return jax.shard_map(body, mesh=mesh, in_specs=in_specs, out_specs=out_specs, check_vma=False)
```

time: 181 us -> 158 us (0.87); the launches traced: 181 us -> 157 us
  Pallas kernels: 82.7 us -> 60.3 us
  other arithmetic: 5.01 us -> 1.7 us
    pallas_call x1, Pallas kernels: 70.6 us -> 49.8 us  [body(): pl.pallas_call(functools.partial(spread_kernel, shards=shards, tiles=tile...]
    pallas_call x1, Pallas kernels: 12.1 us -> 8.84 us  [body(): pl.pallas_call(functools.partial(final_kernel, slabs=slabs, depth=depth,...]
where the time goes in v2:
time: 158 us; the launch traced here: 157 us
  Pallas kernels  60.3 us (38%)
  waiting for transfers between devices  55.7 us (35%)
  blocking collectives  32.8 us (21%)
  starting transfers between devices  5.14 us (3%)
  other arithmetic  1.7 us (1%)
    all_to_all x1, waiting for transfers between devices, body(): lax.all_to_all(spectrum.reshape(slabs, depth * planes, 2 * quarter), 'sla...  55.7 us
    pallas_call x1, Pallas kernels, body(): pl.pallas_call(functools.partial(spread_kernel, shards=shards, tiles=tile...  49.8 us
    all_gather x1, blocking collectives, body(): gathered = lax.all_gather(mine, 'atom', axis=0)  23.1 us
    all_to_all x1, blocking collectives, spread_totals(): shared = lax.all_to_all(sums, ('slab', 'atom'), 0, 0, tiled=True)  9.66 us
    pallas_call x1, Pallas kernels, body(): pl.pallas_call(functools.partial(final_kernel, slabs=slabs, depth=depth,...  8.84 us
    all_to_all x1, starting transfers between devices, body(): lax.all_to_all(spectrum.reshape(slabs, depth * planes, 2 * quarter), 'sla...  5.14 us
  transfers between devices with their start and end apart: 1, of which 1 were waited for; matrix products, arithmetic and copies ran while one was open for 0% of the time, Pallas kernels for 0%

profile of v2, /device:TPU:0, one launch (start us, length us, event | category | flops | bytes accessed | tf_op | source)
XLA Modules:
  0.0 156.5 jit_solution(2906362418097722435)
XLA Ops:
  0.6 1.7 %join.1 = f32[456,128]{1,0:T(8,128)} custom-call(s32[192,128]{1,0:T(8,128)} %bitcast.16, f32[192,128]{1,0:T(8,128)} %bitcast.17, f32[64,128]{1,0:T(8,128)} %charges.1, s32[1,64]{1,0:T(1,128)} %bitcast.21), custom_call_target="tpu_custom_call" | custom-call | tf_op jit(solution)/shard_map/join/pallas_call | solution.py:395
  2.3 23.1 %all-gather.atoms = f32[1824,128]{1,0:T(8,128)S(1)} all-gather(f32[456,128]{1,0:T(8,128)} %join.1), channel_id=2, replica_groups=mesh['slab'=8,'atom'=4] {'atom'}, dimensions={0}, use_global_device_ids=true | all-gather | bytes 1167360 | tf_op jit(solution)/shard_map/all_gather | solution.py:407
  25.4 0.0 copy-start
  25.4 0.6 convert_bitcast_fusion.counts
  26.0 0.3 copy-done
  26.4 49.8 %spread.1 = f32[9472,128]{1,0:T(8,128)} custom-call(s32[4,64]{1,0:T(4,128)} %convert_bitcast_fusion.counts, s32[1]{0:T(128)} %bitcast.1.where_x, f32[1824,128]{1,0:T(8,128)} %copy-done, bf16[4,256,256]{2,1,0:T(8,128)(2,1)} %constant.25.clone.table_x, bf16[512,256]{1,0:T(8,128)(2,1)} %constant.26.clone.high_y, bf16[512,256]{1,0:T(8,128)(2,1)} %constant.27.clone.low_y), custom_call_target="tpu_custom_call" | custom-call | tf_op jit(solution)/shard_map/spread/pallas_call | solution.py:421
  76.1 5.1 %all-to-all-start = ((f32[8,1184,128]{2,1,0:T(8,128)}), f32[8,1184,128]{2,1,0:T(8,128)}, u32[]{:S(2)}, u32[]{:S(2)}) async-start(f32[8,1184,128]{2,1,0:T(8,128)} %bitcast.14), calls=%async_computation | async-start | bytes 9699328 | tf_op jit(solution)/shard_map/all_to_all | solution.py:449
  81.3 0.6 pad_add_fusion.where_k
  81.8 55.7 %all-to-all-done.data = f32[8,1184,128]{2,1,0:T(8,128)} async-done(((f32[8,1184,128]{2,1,0:T(8,128)}), f32[8,1184,128]{2,1,0:T(8,128)}, u32[]{:S(2)}, u32[]{:S(2)}) %all-to-all-start) | async-done | bytes 4849696 | tf_op jit(solution)/shard_map/all_to_all | solution.py:449
  137.5 8.8 %final.1 = (f32[2,32,64,256]{3,2,1,0:T(8,128)}, f32[32,128]{1,0:T(8,128)}) custom-call(s32[2]{0:T(128)} %pad_add_fusion.where_k, f32[3]{0:T(128)} %box.1, f32[8,1184,128]{2,1,0:T(8,128)} %all-to-all-done.data, bf16[256,512]{1,0:T(8,128)(2,1)} %constant.28.clone.table_high, bf16[256,512]{1,0:T(8,128)(2,1)} %constant.29.clone.table_low, ...), custom_call_target="tpu_custom_call" | custom-call | tf_op jit(solution)/shard_map/final/pallas_call | solution.py:456
  146.3 9.7 %all_to_all.17 = f32[32,1,128]{2,1,0:T(1,128)S(1)} all-to-all(f32[32,1,128]{2,1,0:T(1,128)} %bitcast.19), channel_id=1, replica_groups=mesh['slab'=8,'atom'=4] {'slab','atom'}, dimensions={0} | all-to-all | bytes 32768 | tf_op jit(solution)/shard_map/all_to_all | solution.py:500
  156.0 0.5 slice_reduce_fusion
  (1 shorter events, 0.0 us)
Async XLA Ops:
  25.4 0.9 copy-start
  76.1 61.3 %all-to-all-start = ((f32[8,1184,128]{2,1,0:T(8,128)}), f32[8,1184,128]{2,1,0:T(8,128)}, u32[]{:S(2)}, u32[]{:S(2)}) async-start(f32[8,1184,128]{2,1,0:T(8,128)} %bitcast.14), calls=%async_computation | async-start | bytes 9699328 | tf_op jit(solution)/shard_map/all_to_all | solution.py:449

commit v3 on v2

--- a/solution.py
+++ b/solution.py
@@ -110,12 +110,12 @@
 
     n = lax.fori_loop(0, tiles, step, jnp.int32(0))
     packed[pl.ds(tiles * most * 8, 8), :] = jnp.zeros((8, 2 * slots), f32)
-    for g in range(2):
+    for g in range(6):
         items[n + g] = tiles * most
     return n
 
 
-def build_tables(part, left_table, right_table, *, stride, window, depth, rows_tile, group):
+def build_right(part, right_table, factors, *, stride, depth, rows_tile, group):
     taps = spline_taps(part)
     cell = part.astype(jnp.int32)
     weight = part[6:7] * (1.0 / math.factorial(ORDER - 1) ** 3)
@@ -147,8 +147,14 @@
         mask = block == jnp.asarray(b, bf16)
         right_table[pl.ds(b * 16, 16), pl.ds(0, group)] = jnp.where(mask, x_high, none)
         right_table[pl.ds(b * 16, 16), pl.ds(group, group)] = jnp.where(mask, x_low, none)
+    factors[pl.ds(0, stride), :] = along_z
+    factors[pl.ds(stride, 16), :] = along_y
+
+
+def build_left(factors, left_table, *, stride, window, group):
+    along_z = factors[pl.ds(0, stride), :]
     for q in range(0, window, 2):
-        rows = [along_z * along_y[u : u + 1] for u in range(q, min(q + 2, window))]
+        rows = [along_z * factors[pl.ds(stride + u, 1), :] for u in range(q, min(q + 2, window))]
         height = len(rows) * stride
         if height % 16:
             rows.append(jnp.zeros((8, group), f32))
@@ -166,14 +172,19 @@
     high_y,
     low_y,
     out,
-    left,
-    right,
+    grid,
     packed,
     items,
     lt_a,
     rt_a,
+    et_a,
+    zy_a,
     lt_b,
     rt_b,
+    et_b,
+    zy_b,
+    yt_a,
+    yt_b,
     *,
     shards,
     tiles,
@@ -186,61 +197,56 @@
     window = rows_tile + HALO
     group = 2 * slots
     most = shards // 2
-    half = table_x.shape[2] // 2
+    half = table_x.shape[1] // 2
     quarter = half // 2
     step_rows = rows_tile * stride
+    used = window * stride
+    height = lt_a.shape[0]
 
     def clear(t):
-        for ref in (left, right):
-            ref[pl.ds(pl.multiple_of(t * step_rows, 8), step_rows), :] = jnp.zeros((step_rows, K // 2), f32)
-
-    for ref in (left, right):
-        ref[pl.ds(K * stride, HALO * stride), :] = jnp.zeros((HALO * stride, K // 2), f32)
+        grid[pl.ds(pl.multiple_of(t * step_rows, 8), step_rows), :] = jnp.zeros((step_rows, half), f32)
+
+    grid[pl.ds(K * stride, HALO * stride), :] = jnp.zeros((HALO * stride, half), f32)
     count = pack_tiles(counts, atoms, packed, items, clear, shards=shards, tiles=tiles, slots=slots)
-
-    def build(i, lt, rt):
+    phases = table_x[where_x[0]]
+
+    def build(i, rt, zy):
         part = packed[pl.ds(pl.multiple_of(items[i] * 8, 8), 8), :]
-        build_tables(
-            part, lt, rt, stride=stride, window=window, depth=depth, rows_tile=rows_tile, group=group
-        )
-
-    def apply(i, lt, rt):
+        build_right(part, rt, zy, stride=stride, depth=depth, rows_tile=rows_tile, group=group)
+
+    def turn(rt, zy, lt, et):
+        build_left(zy, lt, stride=stride, window=window, group=group)
+        upper = dot(phases, rt[:, :group])
+        lower = dot(phases[:half], rt[:, group:])
+        high, low = split((upper[:half] + lower) + upper[half:])
+        et[pl.ds(0, half), :] = high
+        et[pl.ds(half, half), :] = low
+
+    def apply(i, lt, et):
         t = jnp.minimum(items[i] // most, tiles - 1)
-        lh, ll = lt[:, :group], lt[:, group:]
-        rh, rl = rt[:, :group], rt[:, group:]
-        result = dot_nt(
-            jnp.concatenate([lh, lh, ll], axis=1), jnp.concatenate([rh, rl, rh], axis=1)
-        )
-        at = pl.ds(pl.multiple_of(t * step_rows, 8), window * stride)
-        left[at, :] += result[: window * stride, : K // 2]
-        right[at, :] += result[: window * stride, K // 2 :]
-
-    build(0, lt_a, rt_a)
+        result = dot_nt(jnp.concatenate([lt[:, :group], lt[:, group:]], axis=0), et[...])
+        at = pl.ds(pl.multiple_of(t * step_rows, 8), used)
+        grid[at, :] += (result[:used, half:] + result[height : height + used, :half]) + result[:used, :half]
+
+    build(0, rt_a, zy_a)
+    build(1, rt_b, zy_b)
+    turn(rt_a, zy_a, lt_a, et_a)
+    turn(rt_b, zy_b, lt_b, et_b)
+    build(2, rt_a, zy_a)
+    build(3, rt_b, zy_b)
 
     def pair_step(j, _):
-        apply(2 * j, lt_a, rt_a)
-        build(2 * j + 1, lt_b, rt_b)
-        apply(2 * j + 1, lt_b, rt_b)
-        build(jnp.minimum(2 * j + 2, count), lt_a, rt_a)
+        apply(2 * j, lt_a, et_a)
+        turn(rt_a, zy_a, lt_a, et_a)
+        build(2 * j + 4, rt_a, zy_a)
+        apply(2 * j + 1, lt_b, et_b)
+        turn(rt_b, zy_b, lt_b, et_b)
+        build(2 * j + 5, rt_b, zy_b)
         return 0
 
     lax.fori_loop(0, (count + 1) // 2, pair_step, 0)
-    for ref in (left, right):
-        ref[pl.ds(K * stride, BELOW * stride), :] += ref[pl.ds(0, BELOW * stride), :]
-        ref[pl.ds(BELOW * stride, ABOVE * stride), :] += ref[pl.ds((K + BELOW) * stride, ABOVE * stride), :]
-
-    chunk = 512
-    table = table_x[where_x[0]]
-
-    def x_step(c, _):
-        at = pl.ds(pl.multiple_of(BELOW * stride + c * chunk, 8), chunk)
-        high, low = split(jnp.concatenate([left[at, :], right[at, :]], axis=1))
-        upper = dot(high, table)
-        lower = dot(low, table[:, :half])
-        left[at, :] = (upper[:, :half] + lower) + upper[:, half:]
-        return 0
-
-    lax.fori_loop(0, K * stride // chunk, x_step, 0)
+    grid[pl.ds(K * stride, BELOW * stride), :] += grid[pl.ds(0, BELOW * stride), :]
+    grid[pl.ds(BELOW * stride, ABOVE * stride), :] += grid[pl.ds((K + BELOW) * stride, ABOVE * stride), :]
 
     sign = jnp.where(iota((1, half), 1) < quarter, 1.0, -1.0)
     th, tl = high_y[...], low_y[...]
@@ -251,19 +257,30 @@
 
     table_y = jnp.concatenate([th[:K], th[K:], th[:K], th[K:], tl[:K], tl[K:]], axis=1)
 
-    def plane_pair(first):
-        at = [first, first + 1]
-        data = [left[pl.ds(BELOW * stride + p, K, stride=stride), :] for p in at]
+    def first_of(j):
+        return jnp.minimum(2 * j, planes - 2)
+
+    def load(j, buf):
+        data = [grid[pl.ds(BELOW * stride + first_of(j) + u, K, stride=stride), :] for u in range(2)]
         turned = [pltpu.roll(x, quarter, 1) * sign for x in data]
-        high, low = split(jnp.concatenate(data, axis=1))
-        high_t, low_t = split(jnp.concatenate(turned, axis=1))
-        done = dot(table_y, jnp.concatenate([high, high_t, low, low_t, high, high_t], axis=0))
+        for at, pair in ((0, data), (K, turned)):
+            high, low = split(jnp.concatenate(pair, axis=1))
+            buf[pl.ds(at, K), :] = high
+            buf[pl.ds(at + 2 * K, K), :] = low
+
+    def combine(j, buf):
+        done = dot(table_y, jnp.concatenate([buf[...], buf[pl.ds(0, 2 * K), :]], axis=0))
         for u in range(2):
-            out[pl.ds(slot_of(at[u]), K, stride=planes), :] = done[:, u * half : (u + 1) * half]
+            out[pl.ds(slot_of(first_of(j) + u), K, stride=planes), :] = done[:, u * half : (u + 1) * half]
+
+    load(0, yt_a)
+    load(1, yt_b)
 
     def plane_step(j, _):
-        for u in range(2):
-            plane_pair(jnp.minimum(4 * j + 2 * u, planes - 2))
+        combine(2 * j, yt_a)
+        load(2 * j + 2, yt_a)
+        combine(2 * j + 1, yt_b)
+        load(2 * j + 3, yt_b)
         return 0
 
     lax.fori_loop(0, -(-planes // 4), plane_step, 0)
@@ -411,8 +428,8 @@
     per_x = []
     for i in range(shards):
         part = slice(i * quarter, (i + 1) * quarter)
-        high, low = split_const(np.concatenate([cosine[:, part], -sine[:, part]], axis=1))
-        per_x.append(np.concatenate([high, low], axis=1))
+        high, low = split_const(np.concatenate([cosine[part], -sine[part]], axis=0))
+        per_x.append(np.concatenate([high, low], axis=0))
     table_x = jnp.asarray(np.stack(per_x))
     high_y, low_y = split_const(np.concatenate([cosine, sine], axis=0))
     high_z, low_z = split_const(np.concatenate([cosine, sine], axis=1))
@@ -426,16 +443,18 @@
         in_specs=[smem(), smem(), vmem(), vmem(), vmem(), vmem()],
         out_specs=vmem(),
         scratch_shapes=[
-            pltpu.VMEM(((K + HALO) * stride, K // 2), f32),
-            pltpu.VMEM(((K + HALO) * stride, K // 2), f32),
+            pltpu.VMEM(((K + HALO) * stride, 2 * quarter), f32),
             pltpu.VMEM((tiles * shards * 4 + 8, 2 * slots), f32),
-            pltpu.SMEM((tiles * shards // 2 + shards,), jnp.int32),
+            pltpu.SMEM((tiles * shards // 2 + 8,), jnp.int32),
         ]
         + [
             pltpu.VMEM((-(-(rows_tile + HALO) * stride // 16) * 16, 4 * slots), bf16),
             pltpu.VMEM((K, 4 * slots), bf16),
+            pltpu.VMEM((4 * quarter, 2 * slots), bf16),
+            pltpu.VMEM((stride + 16, 2 * slots), f32),
         ]
-        * 2,
+        * 2
+        + [pltpu.VMEM((4 * K, 4 * quarter), bf16)] * 2,
         compiler_params=pltpu.CompilerParams(vmem_limit_bytes=60 * 1024 * 1024),
         name="spread",
     )(

time: 158 us -> 150 us (0.949)
  Pallas kernels: 60.3 us -> 54.3 us
    pallas_call x1, Pallas kernels: 49.8 us -> 43.8 us  [body(): pl.pallas_call(functools.partial(spread_kernel, shards=shards, tiles=tile...]
where the time goes in v3:
time: 150 us
  waiting for transfers between devices  55.6 us (37%)
  Pallas kernels  54.3 us (36%)
  blocking collectives  32.8 us (22%)
  starting transfers between devices  4.6 us (3%)
  other arithmetic  1.7 us (1%)
    all_to_all x1, waiting for transfers between devices, body(): lax.all_to_all(spectrum.reshape(slabs, depth * planes, 2 * quarter), 'sla...  55.6 us
    pallas_call x1, Pallas kernels, body(): pl.pallas_call(functools.partial(spread_kernel, shards=shards, tiles=tile...  43.8 us
    all_gather x1, blocking collectives, body(): gathered = lax.all_gather(mine, 'atom', axis=0)  23.1 us
    all_to_all x1, blocking collectives, spread_totals(): shared = lax.all_to_all(sums, ('slab', 'atom'), 0, 0, tiled=True)  9.66 us
    pallas_call x1, Pallas kernels, body(): pl.pallas_call(functools.partial(final_kernel, slabs=slabs, depth=depth,...  8.84 us
    all_to_all x1, starting transfers between devices, body(): lax.all_to_all(spectrum.reshape(slabs, depth * planes, 2 * quarter), 'sla...  4.6 us
  transfers between devices with their start and end apart: 1, of which 1 were waited for; matrix products, arithmetic and copies ran while one was open for 0% of the time, Pallas kernels for 0%

profile of v3, /device:TPU:0, one launch (start us, length us, event | category | flops | bytes accessed | tf_op | source)
XLA Modules:
  0.0 149.9 jit_solution(8424597797951497708)
XLA Ops:
  0.6 1.7 %join.1 = f32[456,128]{1,0:T(8,128)} custom-call(s32[192,128]{1,0:T(8,128)} %bitcast.16, f32[192,128]{1,0:T(8,128)} %bitcast.17, f32[64,128]{1,0:T(8,128)} %charges.1, s32[1,64]{1,0:T(1,128)} %bitcast.21), custom_call_target="tpu_custom_call" | custom-call | tf_op jit(solution)/shard_map/join/pallas_call | solution.py:412
  2.3 23.1 %all-gather.atoms = f32[1824,128]{1,0:T(8,128)S(1)} all-gather(f32[456,128]{1,0:T(8,128)} %join.1), channel_id=2, replica_groups=mesh['slab'=8,'atom'=4] {'atom'}, dimensions={0}, use_global_device_ids=true | all-gather | bytes 1167360 | tf_op jit(solution)/shard_map/all_gather | solution.py:424
  25.4 0.0 copy-start
  25.4 0.6 convert_bitcast_fusion.counts
  26.0 0.3 copy-done
  26.4 43.8 %spread.1 = f32[9472,128]{1,0:T(8,128)} custom-call(s32[4,64]{1,0:T(4,128)} %convert_bitcast_fusion.counts, s32[1]{0:T(128)} %bitcast.1.where_x, f32[1824,128]{1,0:T(8,128)} %copy-done, bf16[4,256,256]{2,1,0:T(8,128)(2,1)} %constant.25.clone.table_x, bf16[512,256]{1,0:T(8,128)(2,1)} %constant.26.clone.high_y, bf16[512,256]{1,0:T(8,128)(2,1)} %constant.27.clone.low_y), custom_call_target="tpu_custom_call" | custom-call | tf_op jit(solution)/shard_map/spread/pallas_call | solution.py:438
  70.2 4.6 %all-to-all-start = ((f32[8,1184,128]{2,1,0:T(8,128)}), f32[8,1184,128]{2,1,0:T(8,128)}, u32[]{:S(2)}, u32[]{:S(2)}) async-start(f32[8,1184,128]{2,1,0:T(8,128)} %bitcast.14), calls=%async_computation | async-start | bytes 9699328 | tf_op jit(solution)/shard_map/all_to_all | solution.py:468
  74.8 0.6 pad_add_fusion.where_k
  75.3 55.6 %all-to-all-done.data = f32[8,1184,128]{2,1,0:T(8,128)} async-done(((f32[8,1184,128]{2,1,0:T(8,128)}), f32[8,1184,128]{2,1,0:T(8,128)}, u32[]{:S(2)}, u32[]{:S(2)}) %all-to-all-start) | async-done | bytes 4849696 | tf_op jit(solution)/shard_map/all_to_all | solution.py:468
  130.9 8.8 %final.1 = (f32[2,32,64,256]{3,2,1,0:T(8,128)}, f32[32,128]{1,0:T(8,128)}) custom-call(s32[2]{0:T(128)} %pad_add_fusion.where_k, f32[3]{0:T(128)} %box.1, f32[8,1184,128]{2,1,0:T(8,128)} %all-to-all-done.data, bf16[256,512]{1,0:T(8,128)(2,1)} %constant.28.clone.table_high, bf16[256,512]{1,0:T(8,128)(2,1)} %constant.29.clone.table_low, ...), custom_call_target="tpu_custom_call" | custom-call | tf_op jit(solution)/shard_map/final/pallas_call | solution.py:475
  139.7 9.7 %all_to_all.17 = f32[32,1,128]{2,1,0:T(1,128)S(1)} all-to-all(f32[32,1,128]{2,1,0:T(1,128)} %bitcast.19), channel_id=1, replica_groups=mesh['slab'=8,'atom'=4] {'slab','atom'}, dimensions={0} | all-to-all | bytes 32768 | tf_op jit(solution)/shard_map/all_to_all | solution.py:519
  149.4 0.5 slice_reduce_fusion
  (1 shorter events, 0.0 us)
Async XLA Ops:
  25.4 0.9 copy-start
  70.2 60.7 %all-to-all-start = ((f32[8,1184,128]{2,1,0:T(8,128)}), f32[8,1184,128]{2,1,0:T(8,128)}, u32[]{:S(2)}, u32[]{:S(2)}) async-start(f32[8,1184,128]{2,1,0:T(8,128)} %bitcast.14), calls=%async_computation | async-start | bytes 9699328 | tf_op jit(solution)/shard_map/all_to_all | solution.py:468

commit v4 on v3

--- a/solution.py
+++ b/solution.py
@@ -82,13 +82,14 @@
     out[pl.ds(7 * tiles, 1), pl.ds(0, tiles)] = counts[...].astype(f32)
 
 
-def pack_tiles(counts, atoms, packed, items, clear, *, shards, tiles, slots):
+def pack_tiles(counts, atoms, packed, items, halves, clear, *, shards, tiles, slots):
     fields = 7 * tiles + 8
     most = shards // 2
     lanes = iota((1, slots), 1)
     zero = jnp.zeros((7, slots), f32)
 
-    def step(t, n):
+    def step(t, carry):
+        n, m = carry
         clear(t)
         sums = [zero] * shards
         offset = jnp.int32(0)
@@ -106,13 +107,18 @@
                 [both, jnp.zeros((1, 2 * slots), f32)], axis=0
             )
             items[n + g] = t * most + g
-        return n + (offset + 2 * slots - 1) // (2 * slots)
-
-    n = lax.fori_loop(0, tiles, step, jnp.int32(0))
+        whole = offset // (2 * slots)
+        rest = offset - whole * (2 * slots)
+        halves[m] = t * most + whole
+        m = m + jnp.where((rest > 0) & (rest <= slots), 1, 0)
+        return n + whole + jnp.where(rest > slots, 1, 0), m
+
+    n, m = lax.fori_loop(0, tiles, step, (jnp.int32(0), jnp.int32(0)))
     packed[pl.ds(tiles * most * 8, 8), :] = jnp.zeros((8, 2 * slots), f32)
     for g in range(6):
         items[n + g] = tiles * most
-    return n
+        halves[m + g] = tiles * most
+    return n, m
 
 
 def build_right(part, right_table, factors, *, stride, depth, rows_tile, group):
@@ -175,6 +181,7 @@
     grid,
     packed,
     items,
+    halves,
     lt_a,
     rt_a,
     et_a,
@@ -185,6 +192,14 @@
     zy_b,
     yt_a,
     yt_b,
+    hlt_a,
+    hrt_a,
+    het_a,
+    hzy_a,
+    hlt_b,
+    hrt_b,
+    het_b,
+    hzy_b,
     *,
     shards,
     tiles,
@@ -207,7 +222,7 @@
         grid[pl.ds(pl.multiple_of(t * step_rows, 8), step_rows), :] = jnp.zeros((step_rows, half), f32)
 
     grid[pl.ds(K * stride, HALO * stride), :] = jnp.zeros((HALO * stride, half), f32)
-    count = pack_tiles(counts, atoms, packed, items, clear, shards=shards, tiles=tiles, slots=slots)
+    count, count_half = pack_tiles(counts, atoms, packed, items, halves, clear, shards=shards, tiles=tiles, slots=slots)
     phases = table_x[where_x[0]]
 
     def build(i, rt, zy):
@@ -228,23 +243,50 @@
         at = pl.ds(pl.multiple_of(t * step_rows, 8), used)
         grid[at, :] += (result[:used, half:] + result[height : height + used, :half]) + result[:used, :half]
 
-    build(0, rt_a, zy_a)
-    build(1, rt_b, zy_b)
-    turn(rt_a, zy_a, lt_a, et_a)
-    turn(rt_b, zy_b, lt_b, et_b)
-    build(2, rt_a, zy_a)
-    build(3, rt_b, zy_b)
-
-    def pair_step(j, _):
-        apply(2 * j, lt_a, et_a)
-        turn(rt_a, zy_a, lt_a, et_a)
-        build(2 * j + 4, rt_a, zy_a)
-        apply(2 * j + 1, lt_b, et_b)
-        turn(rt_b, zy_b, lt_b, et_b)
-        build(2 * j + 5, rt_b, zy_b)
-        return 0
-
-    lax.fori_loop(0, (count + 1) // 2, pair_step, 0)
+    def build_half(i, rt, zy):
+        part = packed[pl.ds(pl.multiple_of(halves[i] * 8, 8), 8), pl.ds(0, slots)]
+        build_right(part, rt, zy, stride=stride, depth=depth, rows_tile=rows_tile, group=slots)
+
+    def turn_half(rt, zy, lt, et):
+        build_left(zy, lt, stride=stride, window=window, group=slots)
+        both = dot(phases, rt[...])
+        high, low = split((both[:half, :slots] + both[:half, slots:]) + both[half:, :slots])
+        et[pl.ds(0, half), pl.ds(0, slots)] = high
+        et[pl.ds(0, half), pl.ds(slots, slots)] = high
+        et[pl.ds(half, half), pl.ds(0, slots)] = low
+
+    def apply_half(i, lt, et):
+        t = jnp.minimum(halves[i] // most, tiles - 1)
+        result = dot_nt(lt[...], et[...])
+        at = pl.ds(pl.multiple_of(t * step_rows, 8), used)
+        grid[at, :] += result[:used, half:] + result[:used, :half]
+
+    def run(number, make, shift, add, first, second):
+        (lt, rt, et, zy), (lt2, rt2, et2, zy2) = first, second
+        make(0, rt, zy)
+        make(1, rt2, zy2)
+        shift(rt, zy, lt, et)
+        shift(rt2, zy2, lt2, et2)
+        make(2, rt, zy)
+        make(3, rt2, zy2)
+
+        def pair_step(j, _):
+            add(2 * j, lt, et)
+            shift(rt, zy, lt, et)
+            make(2 * j + 4, rt, zy)
+            add(2 * j + 1, lt2, et2)
+            shift(rt2, zy2, lt2, et2)
+            make(2 * j + 5, rt2, zy2)
+            return 0
+
+        lax.fori_loop(0, (number + 1) // 2, pair_step, 0)
+
+    run(count, build, turn, apply, (lt_a, rt_a, et_a, zy_a), (lt_b, rt_b, et_b, zy_b))
+    for ref in (het_a, het_b):
+        ref[pl.ds(half, half), pl.ds(slots, slots)] = jnp.zeros((half, slots), bf16)
+    run(
+        count_half, build_half, turn_half, apply_half, (hlt_a, hrt_a, het_a, hzy_a), (hlt_b, hrt_b, het_b, hzy_b)
+    )
     grid[pl.ds(K * stride, BELOW * stride), :] += grid[pl.ds(0, BELOW * stride), :]
     grid[pl.ds(BELOW * stride, ABOVE * stride), :] += grid[pl.ds((K + BELOW) * stride, ABOVE * stride), :]
 
@@ -287,11 +329,12 @@
 
 
 def final_kernel(
-    where_k, box, data, table_high, table_low, mod_row, mod_col, field, sums, m_y, g_y, acc, base_zx, sq_zx, *, slabs, depth, quarter, n_dev, norm
+    where_k, box, data, table_high, table_low, mod_row, mod_col, field, sums, m_y, g_y, acc, base_zx, sq_zx, zt_a, zt_b, both_a, both_b, *, slabs, depth, quarter, n_dev, norm
 ):
     planes = depth + HALO
     pair = 4
     here_y = m_y.shape[0]
+    zts, boths = (zt_a, zt_b), (both_a, both_b)
     g = pl.program_id(0)
     scale = math.pi**2 / ewald_beta**2
 
@@ -317,7 +360,7 @@
     g_y[...] = jnp.exp(-scale * rows_y * rows_y) * mod_col[pl.ds(pl.multiple_of(first_y, 8), here_y), :]
     ids = iota((8, 2 * quarter), 0)
 
-    def step(k, _):
+    def load(k, zt):
         tr = []
         for u in range(pair):
             row = (k * pair + u) * planes
@@ -331,15 +374,22 @@
                     ids >= 8 - BELOW, data[(s + 1) % slabs, pl.ds(row + planes - 8, 8), :], 0.0
                 )
                 blocks += [first, mid, last]
-            tr.append(jnp.concatenate(blocks, axis=0).T)
-        high, low = split(jnp.concatenate(tr, axis=0))
+            high, low = split(jnp.concatenate(blocks, axis=0).T)
+            zt[pl.ds(u * 2 * quarter, 2 * quarter), pl.ds(0, K)] = high
+            zt[pl.ds(u * 2 * quarter, 2 * quarter), pl.ds(K, K)] = low
+
+    def transform(zt, both):
         th, tl = table_high[...], table_low[...]
-        both = dot(jnp.concatenate([high, high, low], axis=1), jnp.concatenate([th, tl, th], axis=0))
+        both[...] = dot(
+            jnp.concatenate([zt[...], zt[:, :K]], axis=1), jnp.concatenate([th, th, tl], axis=0)
+        )
+
+    def weigh(k, both):
         for u in range(pair):
             ky = k * pair + u
-            lo, mi, hi = (2 * u * quarter, (2 * u + 1) * quarter, (2 * u + 2) * quarter)
-            real = both[lo:mi, :K] + both[mi:hi, K:]
-            imag = both[mi:hi, :K] - both[lo:mi, K:]
+            lo, hi = pl.ds(2 * u * quarter, quarter), pl.ds((2 * u + 1) * quarter, quarter)
+            real = both[lo, :K] + both[hi, K:]
+            imag = both[hi, :K] - both[lo, K:]
             my = m_y[pl.ds(ky, 1), :]
             msq = sq_zx[...] + my * my
             anchor = msq == 0.0
@@ -356,9 +406,15 @@
             acc[1] += gain
             acc[2] += gy
             acc[3] += gy * my
-        return 0
-
-    lax.fori_loop(0, here_y // pair, step, 0)
+
+    steps = here_y // pair
+    for k in range(steps + 2):
+        if k >= 2:
+            weigh(k - 2, boths[k % 2])
+        if 1 <= k <= steps:
+            transform(zts[(k - 1) % 2], boths[(k - 1) % 2])
+        if k < steps:
+            load(k, zts[k % 2])
 
     @pl.when(g == pl.num_programs(0) - 1)
     def _():
@@ -446,6 +502,7 @@
             pltpu.VMEM(((K + HALO) * stride, 2 * quarter), f32),
             pltpu.VMEM((tiles * shards * 4 + 8, 2 * slots), f32),
             pltpu.SMEM((tiles * shards // 2 + 8,), jnp.int32),
+            pltpu.SMEM((tiles + 8,), jnp.int32),
         ]
         + [
             pltpu.VMEM((-(-(rows_tile + HALO) * stride // 16) * 16, 4 * slots), bf16),
@@ -454,7 +511,14 @@
             pltpu.VMEM((stride + 16, 2 * slots), f32),
         ]
         * 2
-        + [pltpu.VMEM((4 * K, 4 * quarter), bf16)] * 2,
+        + [pltpu.VMEM((4 * K, 4 * quarter), bf16)] * 2
+        + [
+            pltpu.VMEM((-(-(rows_tile + HALO) * stride // 16) * 16, 2 * slots), bf16),
+            pltpu.VMEM((K, 2 * slots), bf16),
+            pltpu.VMEM((4 * quarter, 2 * slots), bf16),
+            pltpu.VMEM((stride + 16, slots), f32),
+        ]
+        * 2,
         compiler_params=pltpu.CompilerParams(vmem_limit_bytes=60 * 1024 * 1024),
         name="spread",
     )(
@@ -469,7 +533,7 @@
         spectrum.reshape(slabs, depth * planes, 2 * quarter), "slab", 0, 0, tiled=True
     )
     mod = moduli_const()
-    block_y = 8
+    block_y = 16
     if depth % 16:
         return plain_final(moved, box, high_z, a, s, slabs, depth, quarter, norm)
     field, sums = pl.pallas_call(
@@ -500,7 +564,9 @@
             pltpu.VMEM((4, quarter, K), f32),
             pltpu.VMEM((quarter, K), f32),
             pltpu.VMEM((quarter, K), f32),
-        ],
+        ]
+        + [pltpu.VMEM((8 * quarter, 2 * K), bf16)] * 2
+        + [pltpu.VMEM((8 * quarter, 2 * K), f32)] * 2,
         compiler_params=pltpu.CompilerParams(vmem_limit_bytes=60 * 1024 * 1024),
         name="final",
     )(

time: 150 us -> 147 us (0.980)
  Pallas kernels: 54.3 us -> 51.6 us
    pallas_call x1, Pallas kernels: 43.8 us -> 41.7 us  [body(): pl.pallas_call(functools.partial(spread_kernel, shards=shards, tiles=tile...]
where the time goes in v4:
time: 147 us
  waiting for transfers between devices  55.6 us (38%)
  Pallas kernels  51.6 us (35%)
  blocking collectives  32.8 us (22%)
  starting transfers between devices  4.6 us (3%)
  other arithmetic  1.7 us (1%)
    all_to_all x1, waiting for transfers between devices, body(): lax.all_to_all(spectrum.reshape(slabs, depth * planes, 2 * quarter), 'sla...  55.6 us
    pallas_call x1, Pallas kernels, body(): pl.pallas_call(functools.partial(spread_kernel, shards=shards, tiles=tile...  41.7 us
    all_gather x1, blocking collectives, body(): gathered = lax.all_gather(mine, 'atom', axis=0)  23.1 us
    all_to_all x1, blocking collectives, spread_totals(): shared = lax.all_to_all(sums, ('slab', 'atom'), 0, 0, tiled=True)  9.66 us
    pallas_call x1, Pallas kernels, body(): pl.pallas_call(functools.partial(final_kernel, slabs=slabs, depth=depth,...  8.33 us
    all_to_all x1, starting transfers between devices, body(): lax.all_to_all(spectrum.reshape(slabs, depth * planes, 2 * quarter), 'sla...  4.6 us
  transfers between devices with their start and end apart: 1, of which 1 were waited for; matrix products, arithmetic and copies ran while one was open for 0% of the time, Pallas kernels for 0%

profile of v4, /device:TPU:0, one launch (start us, length us, event | category | flops | bytes accessed | tf_op | source)
XLA Modules:
  0.0 147.3 jit_solution(11867761327710625563)
XLA Ops:
  0.6 1.7 %join.1 = f32[456,128]{1,0:T(8,128)} custom-call(s32[192,128]{1,0:T(8,128)} %bitcast.16, f32[192,128]{1,0:T(8,128)} %bitcast.17, f32[64,128]{1,0:T(8,128)} %charges.1, s32[1,64]{1,0:T(1,128)} %bitcast.21), custom_call_target="tpu_custom_call" | custom-call | tf_op jit(solution)/shard_map/join/pallas_call | solution.py:468
  2.3 23.1 %all-gather.atoms = f32[1824,128]{1,0:T(8,128)S(1)} all-gather(f32[456,128]{1,0:T(8,128)} %join.1), channel_id=2, replica_groups=mesh['slab'=8,'atom'=4] {'atom'}, dimensions={0}, use_global_device_ids=true | all-gather | bytes 1167360 | tf_op jit(solution)/shard_map/all_gather | solution.py:480
  25.4 0.0 copy-start
  25.4 0.6 convert_bitcast_fusion.counts
  26.0 0.3 copy-done
  26.4 41.7 %spread.1 = f32[9472,128]{1,0:T(8,128)} custom-call(s32[4,64]{1,0:T(4,128)} %convert_bitcast_fusion.counts, s32[1]{0:T(128)} %bitcast.1.where_x, f32[1824,128]{1,0:T(8,128)} %copy-done, bf16[4,256,256]{2,1,0:T(8,128)(2,1)} %constant.25.clone.table_x, bf16[512,256]{1,0:T(8,128)(2,1)} %constant.26.clone.high_y, bf16[512,256]{1,0:T(8,128)(2,1)} %constant.27.clone.low_y), custom_call_target="tpu_custom_call" | custom-call | tf_op jit(solution)/shard_map/spread/pallas_call | solution.py:494
  68.0 4.6 %all-to-all-start = ((f32[8,1184,128]{2,1,0:T(8,128)}), f32[8,1184,128]{2,1,0:T(8,128)}, u32[]{:S(2)}, u32[]{:S(2)}) async-start(f32[8,1184,128]{2,1,0:T(8,128)} %bitcast.14), calls=%async_computation | async-start | bytes 9699328 | tf_op jit(solution)/shard_map/all_to_all | solution.py:532
  72.6 0.6 pad_add_fusion.where_k
  73.2 55.6 %all-to-all-done.data = f32[8,1184,128]{2,1,0:T(8,128)} async-done(((f32[8,1184,128]{2,1,0:T(8,128)}), f32[8,1184,128]{2,1,0:T(8,128)}, u32[]{:S(2)}, u32[]{:S(2)}) %all-to-all-start) | async-done | bytes 4849696 | tf_op jit(solution)/shard_map/all_to_all | solution.py:532
  128.7 8.3 %final.1 = (f32[2,32,64,256]{3,2,1,0:T(8,128)}, f32[32,128]{1,0:T(8,128)}) custom-call(s32[2]{0:T(128)} %pad_add_fusion.where_k, f32[3]{0:T(128)} %box.1, f32[8,1184,128]{2,1,0:T(8,128)} %all-to-all-done.data, bf16[256,512]{1,0:T(8,128)(2,1)} %constant.28.clone.table_high, bf16[256,512]{1,0:T(8,128)(2,1)} %constant.29.clone.table_low, ...), custom_call_target="tpu_custom_call" | custom-call | tf_op jit(solution)/shard_map/final/pallas_call | solution.py:539
  137.1 9.7 %all_to_all.17 = f32[32,1,128]{2,1,0:T(1,128)S(1)} all-to-all(f32[32,1,128]{2,1,0:T(1,128)} %bitcast.19), channel_id=1, replica_groups=mesh['slab'=8,'atom'=4] {'slab','atom'}, dimensions={0} | all-to-all | bytes 32768 | tf_op jit(solution)/shard_map/all_to_all | solution.py:585
  146.7 0.5 slice_reduce_fusion
  (1 shorter events, 0.0 us)
Async XLA Ops:
  25.4 0.9 copy-start
  68.0 60.7 %all-to-all-start = ((f32[8,1184,128]{2,1,0:T(8,128)}), f32[8,1184,128]{2,1,0:T(8,128)}, u32[]{:S(2)}, u32[]{:S(2)}) async-start(f32[8,1184,128]{2,1,0:T(8,128)} %bitcast.14), calls=%async_computation | async-start | bytes 9699328 | tf_op jit(solution)/shard_map/all_to_all | solution.py:532
